TPU v7x, 32 devices: a whole 2x2x4 slice. The times are simulated.
32 devices in a mesh: dp: 4 (over y, x), expert: 4 (over z), tensor: 2 (over core).
Axes of the slice: x: 2, y: 2, z: 4, core: 2. Of those that a mesh axis runs over, the one named last changes fastest.
Arguments:
- tokens: bfloat16 [2048, 2048], P(('dp', 'expert'), 'tensor'), may hold values from -6 to 6
- norm_gain: bfloat16 [2048], replicated, may hold values from 0.25 to 1.75
- expert_ids: int32 [2048, 2], P(('dp', 'expert')), may hold values from 0 to 3, all different within a row; in each aligned block of 128 rows (0 to 127, 128 to 255, ...) at most 128 rows name the same one
- gate_codes: int32 [2048, 2], P(('dp', 'expert')), may hold values from 1 to 255
- gate_weights: bfloat16 [4, 7168, 2048], P('expert', ('dp', 'tensor')), may hold values from -0.125 to 0.125
- up_weights: bfloat16 [4, 7168, 2048], P('expert', ('dp', 'tensor')), may hold values from -0.125 to 0.125
- down_weights: bfloat16 [4, 7168, 2048], P('expert', ('dp', 'tensor')), may hold values from -0.0625 to 0.0625
- value_head: bfloat16 [2048, 128], replicated, may hold values from -0.125 to 0.125
- actions: int32 [2048], P(('dp', 'expert')), may hold values from 0 to 127
- rewards: int32 [2048], P(('dp', 'expert')), may hold values from -8 to 8
- trace_codes: int32 [2048], P(('dp', 'expert')), may hold values from 1 to 1024
Outputs:
- action_values: float32 [2048, 128], P(('dp', 'expert'))
- retrace_targets: float32 [2048], P(('dp', 'expert'))
Inputs may be any that keep to these rules, and one draw needn't show every extreme that they name: `expert_ids`: each row names 2 different experts; within the 128 rows of one index pair of dp and expert each expert is named by at most 128 rows, and in some of these blocks one expert by exactly 128.
All inputs are finite; a program needn't handle non-finite values.
Results may differ from a plain program's by a relative error of at most 0.005.
Values may be sent and summed in bfloat16 or wider, within the bound.
A program may use at most 256 MiB of HBM per device.

v0:
```python
import jax
import jax.numpy as jnp
from jax import lax
from jax.experimental import pallas as pl
from jax.experimental.pallas import tpu as pltpu
from jax.sharding import PartitionSpec as P

TOP = 2
STEPS = 128


DISCOUNT = 0.99
EPSILON = 1e-05


def expert_rows(row_block, gate_matrix, lift_matrix, down_matrix):
    gate_value = lax.dot_general(
        row_block, gate_matrix, (((1,), (1,)), ((), ())), preferred_element_type=jnp.float32
    )
    lift_value = lax.dot_general(
        row_block, lift_matrix, (((1,), (1,)), ((), ())), preferred_element_type=jnp.float32
    )
    hidden = (jax.nn.silu(gate_value) * lift_value).astype(jnp.bfloat16)
    return jnp.dot(hidden, down_matrix, preferred_element_type=jnp.float32)


def retrace(action_values, actions, rewards, trace_codes):
    greedy = jnp.max(action_values, axis=1)
    picked = (
        actions[:, None] == jnp.arange(action_values.shape[1], dtype=jnp.int32)[None, :]
    ).astype(jnp.float32)
    taken = jnp.sum(action_values * picked, axis=1)
    trace = trace_codes.astype(jnp.float32) / 1024.0
    reward = rewards.astype(jnp.float32) * 0.25
    greedy = greedy.reshape(-1, STEPS)
    taken = taken.reshape(-1, STEPS)
    trace = trace.reshape(-1, STEPS)
    reward = reward.reshape(-1, STEPS)
    padding = jnp.zeros_like(greedy[:, :1])
    greedy_next = jnp.concatenate([greedy[:, 1:], padding], axis=1)
    taken_next = jnp.concatenate([taken[:, 1:], padding], axis=1)
    trace_next = jnp.concatenate([trace[:, 1:], padding], axis=1)
    driver = reward + DISCOUNT * (greedy_next - trace_next * taken_next)
    log_sums = jnp.cumsum(jnp.log(DISCOUNT * trace), axis=1)
    spans = log_sums[:, None, :] - log_sums[:, :, None]
    upper_mask = (
        jnp.arange(STEPS, dtype=jnp.int32)[None, :] >= jnp.arange(STEPS, dtype=jnp.int32)[:, None]
    )
    weight = jnp.where(upper_mask[None, :, :], jnp.exp(jnp.minimum(spans, 0.0)), 0.0)
    target = jnp.einsum("nts,ns->nt", weight, driver, precision=lax.Precision.HIGHEST)
    return target.reshape(-1)


def per_device_plain(
    tokens,
    norm_gain,
    expert_ids,
    gate_codes,
    gate_weights,
    up_weights,
    down_weights,
    value_head,
    actions,
    rewards,
    trace_codes,
):
    mesh_rows = ("dp", "expert")
    expert = lax.axis_index("expert")
    codes = gate_codes.astype(jnp.float32)
    gate_share = codes / jnp.sum(codes, axis=1, keepdims=True)
    experts = jnp.arange(lax.axis_size("expert"), dtype=jnp.int32)
    share = jnp.sum(
        jnp.where(expert_ids[:, :, None] == experts[None, None, :], gate_share[:, :, None], 0.0),
        axis=1,
    )
    every_share = lax.all_gather(share, mesh_rows, axis=0, tiled=True)
    own_share = lax.dynamic_slice_in_dim(every_share, expert, 1, axis=1)
    full = lax.all_gather(tokens, "tensor", axis=1, tiled=True)
    widened = full.astype(jnp.float32)
    scaling = lax.rsqrt(jnp.mean(widened * widened, axis=1, keepdims=True) + EPSILON)
    normed = (widened * scaling * norm_gain.astype(jnp.float32)[None, :]).astype(jnp.bfloat16)
    gathered = lax.all_gather(normed, mesh_rows, axis=0, tiled=True)
    scored = jnp.dot(down_weights[0], value_head, preferred_element_type=jnp.float32)
    high = scored.astype(jnp.bfloat16)
    low = (scored - high.astype(jnp.float32)).astype(jnp.bfloat16)
    both = jnp.concatenate([high, low], axis=1)
    wide = expert_rows(gathered, gate_weights[0], up_weights[0], both)
    actions_count = value_head.shape[1]
    partial_values = (wide[:, :actions_count] + wide[:, actions_count:]) * own_share
    partial_values = lax.psum_scatter(partial_values, mesh_rows, scatter_dimension=0, tiled=True)
    action_values = lax.psum(partial_values, "tensor")
    retrace_targets = retrace(action_values, actions, rewards, trace_codes)
    return (action_values, retrace_targets)


RING = 4
MESH = pl.DeviceIdType.MESH
TILE = 128
ORDER = (0, 1, 3, 2)


def gray(place):
    return place + (place // 2) * (1 - 2 * (place % 2))


def critic_kernel(
    tokens_ref,
    gain_ref,
    ids_ref,
    codes_ref,
    gate_ref,
    up_ref,
    down_ref,
    head_ref,
    actions_ref,
    rewards_ref,
    trace_ref,
    values_ref,
    targets_ref,
    raw,
    near,
    far,
    gate_buf,
    up_buf,
    down_buf,
    scored_buf,
    hidden_buf,
    partial,
    given,
    sent,
    landed,
    share_buf,
    halves,
    load_sems,
    pair_send,
    pair_recv,
    ring_send,
    ring_recv,
    line_send,
    swap_send,
    swap_recv,
    give_send,
    give_recv,
    back_send,
    back_recv,
):
    dp = lax.axis_index("dp")
    z = lax.axis_index("expert")
    core = lax.axis_index("tensor")
    other = 1 - core
    p = gray(dp)
    rows = tokens_ref.shape[0]
    half_rows = rows // 2
    part = near.shape[-1]
    planes = (z, z + 1 - 2 * (z % 2), jnp.where(z < 2, 2, 1), jnp.where(z < 2, 3, 0))
    wide = tokens_ref.shape[1]
    hidden_units = gate_ref.shape[1]
    actions_count = head_ref.shape[1]

    def device(step_p, step_z, which):
        return (gray((p + step_p) % RING), (z + step_z) % RING, which)

    load_token = pltpu.make_async_copy(tokens_ref, raw.at[core], load_sems.at[0])
    load_down = pltpu.make_async_copy(down_ref.at[0], down_buf, load_sems.at[1])
    load_gate = pltpu.make_async_copy(gate_ref.at[0], gate_buf, load_sems.at[2])
    load_up = pltpu.make_async_copy(up_ref.at[0], up_buf, load_sems.at[3])
    load_token.start()
    load_down.start()
    load_gate.start()
    load_up.start()

    barrier = pltpu.get_barrier_semaphore()
    for step_p in range(RING):
        for step_z in range(RING):
            if (step_p, step_z) != (0, 0):
                pl.semaphore_signal(
                    barrier, inc=1, device_id=device(step_p, step_z, core), device_id_type=MESH
                )
    pl.semaphore_signal(barrier, inc=1, device_id=device(0, 0, other), device_id_type=MESH)
    pl.semaphore_wait(barrier, RING * RING)

    sends = []

    def send(source, target, send_sem, recv_sem, to, condition=None):
        def make():
            return pltpu.make_async_remote_copy(
                src_ref=source,
                dst_ref=target,
                send_sem=send_sem,
                recv_sem=recv_sem,
                device_id=to,
                device_id_type=MESH,
            )

        if condition is None:
            make().start()
        else:
            pl.when(condition)(lambda: make().start())
        sends.append((condition, make))

    def await_in(target, recv_sem):
        pltpu.make_async_remote_copy(
            src_ref=target,
            dst_ref=target,
            send_sem=recv_sem,
            recv_sem=recv_sem,
            device_id=device(0, 0, other),
            device_id_type=MESH,
        ).wait_recv()

    load_token.wait()
    send(raw.at[core], raw.at[core], pair_send.at[0], pair_recv.at[0], device(0, 0, other))
    first_axis = lax.broadcasted_iota(jnp.int32, (rows, rows), 0)
    second_axis = lax.broadcasted_iota(jnp.int32, (rows, rows), 1)
    same = first_axis == second_axis

    def column(row):
        return jnp.sum(jnp.where(same, row, 0.0), axis=1, keepdims=True)

    def row_of(col):
        return jnp.sum(jnp.where(same, col, 0.0), axis=0, keepdims=True)

    codes = codes_ref[...].astype(jnp.float32)
    gate_share = codes / jnp.sum(codes, axis=0, keepdims=True)
    ids = ids_ref[...]
    for expert in range(RING):
        share = jnp.sum(jnp.where(ids == expert, gate_share, 0.0), axis=0, keepdims=True)
        share_buf[expert] = jnp.broadcast_to(column(share), (rows, actions_count))

    await_in(raw.at[other], pair_recv.at[0])
    left = raw[0].astype(jnp.float32)
    right = raw[1].astype(jnp.float32)
    total = jnp.sum(left * left, axis=1, keepdims=True) + jnp.sum(
        right * right, axis=1, keepdims=True
    )
    scaling = lax.rsqrt(total / (2 * wide) + EPSILON)
    gain = gain_ref[...].astype(jnp.float32)
    for number, widened in enumerate((left, right)):
        normed = (widened * scaling * gain[:, number * wide : (number + 1) * wide]).astype(
            jnp.bfloat16
        )
        near[number, z, p] = normed[:, :part]
        far[number, z, p] = normed[:, part:]

    buffers = (near, far)
    half = (pl.ds(0, half_rows), pl.ds(half_rows, half_rows))
    lower, upper = z > 0, z < RING - 1
    inner = jnp.logical_and(lower, upper)

    def block(kind, which, plane, step_f):
        return buffers[kind].at[which, plane, (p + step_f) % RING]

    def around(kind, plane, step_f, by, cut=None):
        source = block(kind, core, plane, step_f)
        seen = plane * 5 + (step_f - by) % RING
        if cut is not None:
            source = source.at[half[cut]]
            seen = plane * 5 + (4 if cut == 1 else 2)
        send(
            source,
            source,
            ring_send.at[kind, seen],
            ring_recv.at[kind, seen],
            device(by, 0, core),
        )

    def along(kind, plane, step_f, to, condition, lane):
        source = block(kind, core, plane, step_f)
        send(
            source,
            source,
            line_send.at[kind, lane, plane * RING + step_f],
            ring_recv.at[kind, plane * 5 + step_f],
            (dp, to, core),
            condition,
        )

    def both_ways(kind, step_f):
        along(kind, z, step_f, z + 1, upper, 0)
        along(kind, z, step_f, z - 1, lower, 1)

    def onward(kind, plane, step_f):
        along(kind, plane, step_f, jnp.where(plane < z, z + 1, z - 1), inner, 0)

    def arrive(kind, plane, step_f, split=False):
        here = block(kind, core, plane, step_f)
        if split:
            await_in(here.at[half[0]], ring_recv.at[kind, plane * 5 + 2])
            await_in(here.at[half[1]], ring_recv.at[kind, plane * 5 + 4])
        else:
            await_in(here, ring_recv.at[kind, plane * 5 + step_f])

    def swap(kind, plane, step_f):
        here = block(kind, core, plane, step_f)
        seen = plane * RING + step_f
        send(
            here,
            here,
            swap_send.at[kind, seen],
            swap_recv.at[kind, seen],
            device(0, 0, other),
        )

    def swapped(kind, plane, step_f):
        await_in(block(kind, other, plane, step_f), swap_recv.at[kind, plane * RING + step_f])

    def turn(kind, plane):
        for step_f in (1, 3):
            arrive(kind, plane, step_f)
            around(kind, plane, step_f, (4 - step_f) % RING, cut=0 if step_f == 3 else 1)
        for step_f in (1, 3):
            swap(kind, plane, step_f)

    def turn_last(kind, plane):
        arrive(kind, plane, 2, split=True)
        swap(kind, plane, 2)

    def passing(step, steps_f):
        for step_f in steps_f:
            arrive(0, planes[step], step_f)
            onward(0, planes[step], step_f)
            swap(0, planes[step], step_f)

    def climb(step):
        plane = planes[step]
        arrive(1, plane, 0)
        onward(1, plane, 0)
        around(1, plane, 0, 1)
        around(1, plane, 0, 3)
        swap(1, plane, 0)

    both_ways(1, 0)
    around(0, z, 0, 1)
    around(0, z, 0, 3)
    both_ways(0, 0)
    around(1, z, 0, 1)
    around(1, z, 0, 3)

    load_down.wait()
    scored = jnp.dot(down_buf[...], head_ref[...], preferred_element_type=jnp.float32)
    high = scored.astype(jnp.bfloat16)
    scored_buf[:, :actions_count] = high
    scored_buf[:, actions_count:] = (scored - high.astype(jnp.float32)).astype(jnp.bfloat16)

    tiles = hidden_units // TILE
    cuts = [tiles * number // 4 for number in range(5)]

    def compute(step):
        begin(step)
        more(step, 1)
        more(step, 2)
        finish(step)

    def begin(step):
        plane = planes[step]
        for step_f in ORDER:
            if step > 0 or step_f > 0:
                swapped(0, plane, step_f)
                swapped(1, plane, step_f)
        tile_span(plane, 0, cuts[1])

    def more(step, number):
        tile_span(planes[step], cuts[number], cuts[number + 1])

    def tile_span(plane, first, last):
        lhs_rows = RING * rows

        def tile(index, carry):
            at = pl.ds(pl.multiple_of(index * TILE, TILE), TILE)
            weights = jnp.concatenate([gate_buf[at, :], up_buf[at, :]], axis=0)
            lhs = jnp.concatenate(
                [
                    buffer[which, plane].reshape(lhs_rows, buffer.shape[-1])
                    for which in range(2)
                    for buffer in buffers
                ],
                axis=1,
            )
            both = lax.dot_general(
                lhs, weights, (((1,), (1,)), ((), ())), preferred_element_type=jnp.float32
            )
            hidden_buf[:, at] = (jax.nn.silu(both[:, :TILE]) * both[:, TILE:]).astype(
                jnp.bfloat16
            )
            return carry

        lax.fori_loop(first, last, tile, 0)

    def finish(step):
        tile_span(planes[step], cuts[3], tiles)
        result = jnp.dot(
            hidden_buf[...], scored_buf[...], preferred_element_type=jnp.float32
        )
        result = result[:, :actions_count] + result[:, actions_count:]
        result = result.reshape(RING, 2, half_rows, actions_count)
        partial[step, 0] = result[:, 0]
        partial[step, 1] = result[:, 1]
        send(
            partial.at[step, other],
            given.at[step],
            give_send.at[step],
            give_recv.at[step],
            device(0, 0, other),
        )

    def give_back(step):
        plane = planes[step]
        await_in(given.at[step], give_recv.at[step])
        sent[step] = (partial[step, core] + given[step]).astype(jnp.bfloat16)
        for step_f in range(RING):
            place = (p + step_f) % RING
            if (step, step_f) == (0, 0):
                landed[z, p] = sent[0, p]
            else:
                send(
                    sent.at[step, place],
                    landed.at[z, p],
                    back_send.at[RING * step + step_f],
                    back_recv.at[z * RING + (-step_f) % RING],
                    (gray(place), plane, core),
                )

    turn(0, z)
    both_ways(0, 1)
    both_ways(0, 3)
    climb(1)
    arrive(0, z, 2, split=True)
    both_ways(0, 2)
    swap(0, z, 2)
    turn(1, z)
    passing(1, (0, 1, 3))
    climb(2)
    turn_last(1, z)
    load_gate.wait()
    load_up.wait()
    begin(0)
    passing(1, (2,))
    more(0, 1)
    turn(1, planes[1])
    more(0, 2)
    passing(2, (0,))
    climb(3)
    finish(0)
    passing(2, (1,))
    turn_last(1, planes[1])
    begin(1)
    passing(2, (3,))
    more(1, 1)
    passing(2, (2,))
    turn(1, planes[2])
    more(1, 2)
    give_back(0)
    passing(3, (0,))
    finish(1)
    passing(3, (1,))
    turn_last(1, planes[2])
    begin(2)
    passing(3, (3,))
    more(2, 1)
    turn(1, planes[3])
    passing(3, (2,))
    more(2, 2)
    give_back(1)
    finish(2)
    turn_last(1, planes[3])
    compute(3)
    give_back(2)
    give_back(3)

    for step in range(RING):
        for step_f in range(RING):
            if (step, step_f) != (0, 0):
                await_in(
                    landed.at[planes[step], (p + step_f) % RING],
                    back_recv.at[planes[step] * RING + step_f],
                )
    mine = pl.ds(pl.multiple_of(core * half_rows, half_rows), half_rows)
    blended = jnp.zeros((half_rows, actions_count), jnp.float32)
    for expert in range(RING):
        part_sum = jnp.zeros((half_rows, actions_count), jnp.float32)
        for place in range(RING):
            part_sum = part_sum + landed[expert, place].astype(jnp.float32)
        blended = blended + share_buf[expert, mine, :] * part_sum
    halves[core] = blended
    send(
        halves.at[core], halves.at[core], pair_send.at[1], pair_recv.at[1], device(0, 0, other)
    )

    trace_row = trace_ref[...].astype(jnp.float32) / 1024.0
    trace_col = column(trace_row)
    reward_col = column(rewards_ref[...].astype(jnp.float32) * 0.25)
    action_col = column(actions_ref[...].astype(jnp.float32))
    log_row = jnp.log(DISCOUNT * trace_row)
    log_col = column(log_row)
    sums_row = jnp.sum(jnp.where(first_axis <= second_axis, log_col, 0.0), axis=0, keepdims=True)
    sums_col = jnp.sum(jnp.where(second_axis <= first_axis, log_row, 0.0), axis=1, keepdims=True)
    weight = jnp.where(
        first_axis >= second_axis, jnp.exp(jnp.minimum(sums_col - sums_row, 0.0)), 0.0
    )
    action_axis = lax.broadcasted_iota(jnp.int32, (rows, actions_count), 1).astype(jnp.float32)
    chosen = action_axis == action_col

    await_in(halves.at[other], pair_recv.at[1])
    values = jnp.concatenate([halves[0], halves[1]], axis=0)
    values_ref[...] = values
    greedy = jnp.max(values, axis=1, keepdims=True)
    taken = jnp.sum(jnp.where(chosen, values, 0.0), axis=1, keepdims=True)
    ahead_row = row_of(greedy - trace_col * taken)
    ahead = jnp.sum(
        jnp.where(second_axis == first_axis + 1, ahead_row, 0.0), axis=1, keepdims=True
    )
    driver = reward_col + DISCOUNT * ahead
    targets_ref[...] = jnp.sum(weight * driver, axis=0, keepdims=True)
    for condition, make in sends:
        if condition is None:
            make().wait_send()
        else:
            pl.when(condition)(lambda make=make: make().wait_send())


def per_device(
    tokens,
    norm_gain,
    expert_ids,
    gate_codes,
    gate_weights,
    up_weights,
    down_weights,
    value_head,
    actions,
    rewards,
    trace_codes,
):
    rows, wide = tokens.shape
    hidden_units, features = gate_weights.shape[1:]
    actions_count = value_head.shape[1]
    part = wide // 4
    held = (2, RING, RING, rows)
    half_rows = rows // 2
    vmem = pl.BlockSpec(memory_space=pltpu.VMEM)
    hbm = pl.BlockSpec(memory_space=pltpu.HBM)
    dma = pltpu.SemaphoreType.DMA
    blocks = RING * RING
    values, targets = pl.pallas_call(
        critic_kernel,
        out_shape=(
            jax.ShapeDtypeStruct((rows, actions_count), jnp.float32),
            jax.ShapeDtypeStruct((1, rows), jnp.float32),
        ),
        in_specs=[hbm, vmem, vmem, vmem, hbm, hbm, hbm, vmem, vmem, vmem, vmem],
        out_specs=(vmem, vmem),
        scratch_shapes=[
            pltpu.VMEM((2, rows, wide), jnp.bfloat16),
            pltpu.VMEM((*held, part), jnp.bfloat16),
            pltpu.VMEM((*held, wide - part), jnp.bfloat16),
            pltpu.VMEM((hidden_units, features), jnp.bfloat16),
            pltpu.VMEM((hidden_units, features), jnp.bfloat16),
            pltpu.VMEM((hidden_units, features), jnp.bfloat16),
            pltpu.VMEM((hidden_units, 2 * actions_count), jnp.bfloat16),
            pltpu.VMEM((RING * rows, hidden_units), jnp.bfloat16),
            pltpu.VMEM((RING, 2, RING, half_rows, actions_count), jnp.float32),
            pltpu.VMEM((RING, RING, half_rows, actions_count), jnp.float32),
            pltpu.VMEM((RING, RING, half_rows, actions_count), jnp.bfloat16),
            pltpu.VMEM((RING, RING, half_rows, actions_count), jnp.bfloat16),
            pltpu.VMEM((RING, rows, actions_count), jnp.float32),
            pltpu.VMEM((2, rows // 2, actions_count), jnp.float32),
            dma((4,)),
            dma((2,)),
            dma((2,)),
            dma((2, 5 * RING)),
            dma((2, 5 * RING)),
            dma((2, 2, blocks)),
            dma((2, blocks)),
            dma((2, blocks)),
            dma((RING,)),
            dma((RING,)),
            dma((blocks,)),
            dma((blocks,)),
        ],
        compiler_params=pltpu.CompilerParams(
            collective_id=0, has_side_effects=True, vmem_limit_bytes=60 * 1024 * 1024
        ),
    )(
        tokens,
        norm_gain.reshape(1, -1),
        expert_ids.T,
        gate_codes.T,
        gate_weights,
        up_weights,
        down_weights,
        value_head,
        actions.reshape(1, -1),
        rewards.reshape(1, -1),
        trace_codes.reshape(1, -1),
    )
    return values, targets.reshape(-1)


def solution(mesh):
    in_specs = (
        P(("dp", "expert"), "tensor"),
        P(),
        P(("dp", "expert"), None),
        P(("dp", "expert"), None),
        P("expert", ("dp", "tensor"), None),
        P("expert", ("dp", "tensor"), None),
        P("expert", ("dp", "tensor"), None),
        P(),
        P(("dp", "expert")),
        P(("dp", "expert")),
        P(("dp", "expert")),
    )
    out_specs = (P(("dp", "expert"), None), P(("dp", "expert")))
    shape = mesh.shape
    rings = shape["dp"] == RING and shape["expert"] == RING and shape["tensor"] == 2
    body = per_device if rings else per_device_plain
    return jax.shard_map(
        body, mesh=mesh, in_specs=in_specs, out_specs=out_specs, check_vma=False
    )
```

profile of v0, /device:TPU:1, one launch (start us, length us, event | category | flops | bytes accessed | tf_op | source)
XLA Modules:
  0.0 76.3 jit_solution(17501294486678502851)
XLA Ops:
  0.6 1.3 %reshape.19.gain_ref = bf16[1,2048]{1,0:T(2,128)(2,1)} reshape(bf16[2048]{0:T(1024)(128)(2,1)} %param.12) | data formatting | bytes 8192 | tf_op jit(solution)/shard_map/reshape | solution.py:585
  1.9 71.8 %shard_map.122 = (f32[128,128]{1,0:T(8,128)}, f32[1,128]{1,0:T(1,128)}) custom-call(bf16[128,1024]{1,0:T(8,128)(2,1)} %tokens_ref.1, bf16[1,2048]{1,0:T(2,128)(2,1)} %reshape.19.gain_ref, s32[2,128]{1,0:T(2,128)} %bitcast.6, s32[2,128]{1,0:T(2,128)} %bitcast.7, bf16[1,896,2048]{2,1,0:T(8,128)(2,1)} %gate_ref.1, bf16[1,896,2048]{2,1,0:T(8,128)(2,1)} %up_ref.1, ...), custom_call_target="tpu_custom_call" | custom-call | tf_op jit(solution)/shard_map/pallas_call | solution.py:544
  73.8 1.5 %copy.15 = f32[128,128]{1,0:T(8,128)} copy(f32[128,128]{1,0:T(8,128)} %get-tuple-element.8) | data formatting | bytes 131072
  75.2 1.1 %copy.16 = f32[128]{0:T(128)} copy(f32[128]{0:T(128)} %bitcast.11) | data formatting | bytes 1024
where the time goes:
time: 76.6 us; the launch traced here: 76.3 us
  Pallas kernels  71.8 us (94%)
  local copies, waits for them, and re-layouts  3.88 us (5%)
    pallas_call x1, Pallas kernels, per_device(): pl.pallas_call(critic_kernel, out_shape=(jax.ShapeDtypeStruct((rows, acti...  71.8 us
    unnamed x2, local copies, waits for them, and re-layouts  2.59 us

commit v1 on v0

v1 whole, which is shorter than its diff:
```python
import jax
import jax.numpy as jnp
from jax import lax
from jax.experimental import pallas as pl
from jax.experimental.pallas import tpu as pltpu
from jax.sharding import PartitionSpec as P

TOP = 2
STEPS = 128


DISCOUNT = 0.99
EPSILON = 1e-05


def expert_rows(row_block, gate_matrix, lift_matrix, down_matrix):
    gate_value = lax.dot_general(
        row_block, gate_matrix, (((1,), (1,)), ((), ())), preferred_element_type=jnp.float32
    )
    lift_value = lax.dot_general(
        row_block, lift_matrix, (((1,), (1,)), ((), ())), preferred_element_type=jnp.float32
    )
    hidden = (jax.nn.silu(gate_value) * lift_value).astype(jnp.bfloat16)
    return jnp.dot(hidden, down_matrix, preferred_element_type=jnp.float32)


def retrace(action_values, actions, rewards, trace_codes):
    greedy = jnp.max(action_values, axis=1)
    picked = (
        actions[:, None] == jnp.arange(action_values.shape[1], dtype=jnp.int32)[None, :]
    ).astype(jnp.float32)
    taken = jnp.sum(action_values * picked, axis=1)
    trace = trace_codes.astype(jnp.float32) / 1024.0
    reward = rewards.astype(jnp.float32) * 0.25
    greedy = greedy.reshape(-1, STEPS)
    taken = taken.reshape(-1, STEPS)
    trace = trace.reshape(-1, STEPS)
    reward = reward.reshape(-1, STEPS)
    padding = jnp.zeros_like(greedy[:, :1])
    greedy_next = jnp.concatenate([greedy[:, 1:], padding], axis=1)
    taken_next = jnp.concatenate([taken[:, 1:], padding], axis=1)
    trace_next = jnp.concatenate([trace[:, 1:], padding], axis=1)
    driver = reward + DISCOUNT * (greedy_next - trace_next * taken_next)
    log_sums = jnp.cumsum(jnp.log(DISCOUNT * trace), axis=1)
    spans = log_sums[:, None, :] - log_sums[:, :, None]
    upper_mask = (
        jnp.arange(STEPS, dtype=jnp.int32)[None, :] >= jnp.arange(STEPS, dtype=jnp.int32)[:, None]
    )
    weight = jnp.where(upper_mask[None, :, :], jnp.exp(jnp.minimum(spans, 0.0)), 0.0)
    target = jnp.einsum("nts,ns->nt", weight, driver, precision=lax.Precision.HIGHEST)
    return target.reshape(-1)


def per_device_plain(
    tokens,
    norm_gain,
    expert_ids,
    gate_codes,
    gate_weights,
    up_weights,
    down_weights,
    value_head,
    actions,
    rewards,
    trace_codes,
):
    mesh_rows = ("dp", "expert")
    expert = lax.axis_index("expert")
    codes = gate_codes.astype(jnp.float32)
    gate_share = codes / jnp.sum(codes, axis=1, keepdims=True)
    experts = jnp.arange(lax.axis_size("expert"), dtype=jnp.int32)
    share = jnp.sum(
        jnp.where(expert_ids[:, :, None] == experts[None, None, :], gate_share[:, :, None], 0.0),
        axis=1,
    )
    every_share = lax.all_gather(share, mesh_rows, axis=0, tiled=True)
    own_share = lax.dynamic_slice_in_dim(every_share, expert, 1, axis=1)
    full = lax.all_gather(tokens, "tensor", axis=1, tiled=True)
    widened = full.astype(jnp.float32)
    scaling = lax.rsqrt(jnp.mean(widened * widened, axis=1, keepdims=True) + EPSILON)
    normed = (widened * scaling * norm_gain.astype(jnp.float32)[None, :]).astype(jnp.bfloat16)
    gathered = lax.all_gather(normed, mesh_rows, axis=0, tiled=True)
    scored = jnp.dot(down_weights[0], value_head, preferred_element_type=jnp.float32)
    high = scored.astype(jnp.bfloat16)
    low = (scored - high.astype(jnp.float32)).astype(jnp.bfloat16)
    both = jnp.concatenate([high, low], axis=1)
    wide = expert_rows(gathered, gate_weights[0], up_weights[0], both)
    actions_count = value_head.shape[1]
    partial_values = (wide[:, :actions_count] + wide[:, actions_count:]) * own_share
    partial_values = lax.psum_scatter(partial_values, mesh_rows, scatter_dimension=0, tiled=True)
    action_values = lax.psum(partial_values, "tensor")
    retrace_targets = retrace(action_values, actions, rewards, trace_codes)
    return (action_values, retrace_targets)


RING = 4
MESH = pl.DeviceIdType.MESH
TILE = 128
COMPUTE = True
PIECES = {"W": 0, "N": 0, "a": 0, "b": 1, "A": 2, "B": 3}


def gray(place):
    return place + (place // 2) * (1 - 2 * (place % 2))


def critic_kernel(
    tokens_ref,
    gain_ref,
    ids_ref,
    codes_ref,
    gate_ref,
    up_ref,
    down_ref,
    head_ref,
    actions_ref,
    rewards_ref,
    trace_ref,
    values_ref,
    targets_ref,
    raw,
    held,
    gate_buf,
    up_buf,
    down_buf,
    turned,
    scored_buf,
    hidden_buf,
    squares,
    scale_rows,
    scale_cols,
    near_part,
    far_part,
    near_given,
    far_given,
    near_sent,
    far_sent,
    near_landed,
    far_landed,
    share_buf,
    halves,
    load_sems,
    pair_send,
    pair_recv,
    move_send,
    move_recv,
    swap_send,
    swap_recv,
    scale_recv,
    give_send,
    give_recv,
    back_send,
    back_recv,
):
    dp = lax.axis_index("dp")
    z = lax.axis_index("expert")
    core = lax.axis_index("tensor")
    other = 1 - core
    p = gray(dp)
    rows, wide = tokens_ref.shape
    hidden_units = gate_ref.shape[1]
    actions_count = head_ref.shape[1]
    near = rows // 4
    near_half = near // 2
    far_half = (rows - near) // 2
    spans = {
        "W": (0, rows),
        "N": (0, near),
        "F": (near, rows - near),
        "a": (0, near_half),
        "b": (near_half, near_half),
        "A": (near, far_half),
        "B": (near + far_half, far_half),
    }
    inward = jnp.where(z < RING // 2, 1, -1)
    at_end = jnp.logical_or(z == 0, z == RING - 1)
    inner = jnp.logical_not(at_end)
    planes = (
        z,
        jnp.where(at_end, z + inward, z - inward),
        jnp.where(at_end, z + 2 * inward, z + inward),
        jnp.where(at_end, z + 3 * inward, z + 2 * inward),
    )

    def device(step_p, plane, which):
        return (gray((p + step_p) % RING), plane, which)

    load_token = pltpu.make_async_copy(tokens_ref, raw, load_sems.at[0])
    load_gate = pltpu.make_async_copy(gate_ref.at[0], gate_buf, load_sems.at[1])
    load_up = pltpu.make_async_copy(up_ref.at[0], up_buf, load_sems.at[2])
    load_down = pltpu.make_async_copy(down_ref.at[0], down_buf, load_sems.at[3])
    load_token.start()
    load_gate.start()
    load_up.start()
    load_down.start()

    barrier = pltpu.get_barrier_semaphore()

    def greet(to):
        pl.semaphore_signal(barrier, inc=1, device_id=to, device_id_type=MESH)

    greet(device(0, z, other))
    greet(device(1, z, core))
    greet(device(3, z, core))
    greet(device(0, z + inward, core))
    pl.when(inner)(lambda: greet(device(0, z - inward, core)))

    sends = []
    group = [None]
    held_back = []
    mover = {None: 0, "end": 0, "inner": 0}

    def make_send(source, target, send_sem, recv_sem, to):
        def make():
            return pltpu.make_async_remote_copy(
                src_ref=source,
                dst_ref=target,
                send_sem=send_sem,
                recv_sem=recv_sem,
                device_id=to,
                device_id_type=MESH,
            )

        sends.append((group[0], make))
        act(lambda: make().start())

    def await_in(target, recv_sem):
        sibling = device(0, z, other)
        act(
            lambda: pltpu.make_async_remote_copy(
                src_ref=target,
                dst_ref=target,
                send_sem=recv_sem,
                recv_sem=recv_sem,
                device_id=sibling,
                device_id_type=MESH,
            ).wait_recv()
        )

    def act(step):
        if group[0] is None:
            step()
        else:
            held_back.append(step)

    def only(which, body):
        group[0] = which
        body()
        group[0] = None
        steps = list(held_back)
        held_back.clear()

        def run():
            for step in steps:
                step()

        pl.when(at_end if which == "end" else inner)(run)

    def piece(which, step, step_f, kind):
        first, count = spans[kind]
        return held.at[which, planes[step], (p + step_f) % RING, pl.ds(first, count)]

    def move_sem():
        number = mover[group[0]]
        mover[group[0]] += 1
        if group[0] is None:
            return move_send.at[0, number]
        return move_send.at[1, number]

    def around(step, step_f, kind, by):
        here = piece(core, step, step_f, kind)
        seen = move_recv.at[planes[step], (step_f - by) % RING, PIECES[kind]]
        make_send(here, here, move_sem(), seen, device(by, z, core))
        if kind == "A" and (step, step_f) != (0, 0):
            send_scale(step, step_f, by, z)

    def along(step, step_f, kind, plane):
        here = piece(core, step, step_f, kind)
        seen = move_recv.at[planes[step], step_f, PIECES[kind]]
        make_send(here, here, move_sem(), seen, device(0, plane, core))
        if kind == "A" and (step, step_f) != (0, 0):
            send_scale(step, step_f, 0, plane)

    def send_scale(step, step_f, by, plane):
        here = scale_rows.at[planes[step], (p + step_f) % RING]
        seen = scale_recv.at[planes[step], (step_f - by) % RING]
        make_send(here, here, move_sem(), seen, device(by, plane, core))

    def inwards(step, step_f, kind):
        along(step, step_f, kind, z + inward)

    def outwards(step, step_f, kind):
        along(step, step_f, kind, z - inward)

    def arrive(step, step_f, kind):
        await_in(
            piece(core, step, step_f, kind),
            move_recv.at[planes[step], step_f, PIECES[kind]],
        )
        if kind == "A":
            await_in(
                scale_rows.at[planes[step], (p + step_f) % RING],
                scale_recv.at[planes[step], step_f],
            )

    def swap(step, step_f, kind):
        here = piece(core, step, step_f, kind)
        seen = (planes[step], step_f, PIECES[kind])
        make_send(here, here, swap_send.at[seen], swap_recv.at[seen], device(0, z, other))

    def take(step, step_f, kind):
        arrive(step, step_f, kind)
        swap(step, step_f, kind)

    def swapped(step, step_f, kind):
        await_in(
            piece(other, step, step_f, kind),
            swap_recv.at[planes[step], step_f, PIECES[kind]],
        )

    first_axis = lax.broadcasted_iota(jnp.int32, (rows, rows), 0)
    second_axis = lax.broadcasted_iota(jnp.int32, (rows, rows), 1)
    same = first_axis == second_axis

    def column(row):
        return jnp.sum(jnp.where(same, row, 0.0), axis=1, keepdims=True)

    def row_of(col):
        return jnp.sum(jnp.where(same, col, 0.0), axis=0, keepdims=True)

    load_token.wait()
    widened = raw[...].astype(jnp.float32)
    gain = gain_ref[:, pl.ds(pl.multiple_of(core * wide, wide), wide)].astype(jnp.float32)
    held[core, z, p] = (widened * gain).astype(jnp.bfloat16)
    pl.semaphore_wait(barrier, jnp.where(at_end, 4, 5))

    around(0, 0, "N", 1)
    around(0, 0, "N", 3)
    inwards(0, 0, "A")
    only("inner", lambda: outwards(0, 0, "A"))
    around(0, 0, "A", 1)
    around(0, 0, "B", 3)
    inwards(0, 0, "B")
    only("inner", lambda: outwards(0, 0, "B"))
    swap(0, 0, "W")
    only("end", lambda: inwards(0, 0, "N"))

    squares[core] = row_of(jnp.sum(widened * widened, axis=1, keepdims=True))
    make_send(
        squares.at[core], squares.at[core], pair_send.at[0], pair_recv.at[0], device(0, z, other)
    )

    codes = codes_ref[...].astype(jnp.float32)
    gate_share = codes / jnp.sum(codes, axis=0, keepdims=True)
    ids = ids_ref[...]
    for expert in range(RING):
        share = jnp.sum(jnp.where(ids == expert, gate_share, 0.0), axis=0, keepdims=True)
        share_buf[expert] = jnp.broadcast_to(column(share), (rows, actions_count))

    await_in(squares.at[other], pair_recv.at[0])
    total = squares[0] + squares[1]
    scale_rows[z, p] = lax.rsqrt(total / (2 * wide) + EPSILON)
    send_scale(0, 0, 1, z)
    send_scale(0, 0, 3, z)
    send_scale(0, 0, 0, z + inward)
    only("inner", lambda: send_scale(0, 0, 0, z - inward))

    def turn(tile):
        at = tile * TILE
        turned[:, 2 * at : 2 * at + TILE] = gate_buf[at : at + TILE, :].T
        turned[:, 2 * at + TILE : 2 * at + 2 * TILE] = up_buf[at : at + TILE, :].T

    def scale_of(step, step_f):
        place = (p + step_f) % RING
        scale_cols[step, step_f] = jnp.broadcast_to(
            column(scale_rows[planes[step], place]), (rows, TILE)
        )

    scaled = set()

    def chunk(*items):
        parts = []
        for step, step_f, kind in items:
            if (step, step_f) not in scaled:
                scaled.add((step, step_f))
                scale_of(step, step_f)
            if (step, step_f) == (0, 0):
                swapped(0, 0, "W")
            elif kind == "W":
                for part in "NAB":
                    swapped(step, step_f, part)
            elif kind == "F":
                swapped(step, step_f, "A")
                swapped(step, step_f, "B")
            else:
                swapped(step, step_f, "N")
            parts.append((planes[step], (p + step_f) % RING, *spans[kind]))
        count = sum(part[3] for part in parts)
        scale = jnp.concatenate(
            [
                scale_cols[step, step_f, spans[kind][0] : sum(spans[kind])]
                for step, step_f, kind in items
            ],
            axis=0,
        )
        for tile in range(hidden_units // TILE if COMPUTE else 0):
            at = tile * TILE
            lhs = jnp.concatenate(
                [
                    jnp.concatenate(
                        [
                            held[which, plane, place, first : first + number]
                            for plane, place, first, number in parts
                        ],
                        axis=0,
                    )
                    for which in range(2)
                ],
                axis=1,
            )
            both = jnp.dot(
                lhs, turned[:, 2 * at : 2 * at + 2 * TILE], preferred_element_type=jnp.float32
            )
            hidden_buf[:count, at : at + TILE] = (
                jax.nn.silu(both[:, :TILE] * scale) * (both[:, TILE:] * scale)
            ).astype(jnp.bfloat16)
        result = jnp.dot(
            hidden_buf[:count, :], scored_buf[...], preferred_element_type=jnp.float32
        )
        result = result[:, :actions_count] + result[:, actions_count:]
        offset = 0
        for step, step_f, kind in items:
            if kind in "WN":
                near_part[step, step_f, 0] = result[offset : offset + near_half]
                near_part[step, step_f, 1] = result[offset + near_half : offset + near]
                offset += near
            if kind in "WF":
                far_part[step, step_f, 0] = result[offset : offset + far_half]
                far_part[step, step_f, 1] = result[offset + far_half : offset + 2 * far_half]
                offset += 2 * far_half
        for step, step_f, kind in items:
            for number, part, given in buffers_of(kind):
                at = 2 * (RING * step + step_f) + number
                make_send(
                    part.at[step, step_f, other],
                    given.at[step, step_f],
                    give_send.at[at],
                    give_recv.at[at],
                    device(0, z, other),
                )

    def buffers_of(kind):
        if kind in "WN":
            yield 0, near_part, near_given
        if kind in "WF":
            yield 1, far_part, far_given

    def give_back(*items):
        for step, step_f, kind in items:
            for number, part, given in buffers_of(kind):
                sent, landed = ((near_sent, near_landed), (far_sent, far_landed))[number]
                at = 2 * (RING * step + step_f) + number
                await_in(given.at[step, step_f], give_recv.at[at])
                total = (part[step, step_f, core] + given[step, step_f]).astype(jnp.bfloat16)
                if (step, step_f) == (0, 0):
                    landed[z, p] = total
                else:
                    sent[step, step_f] = total
                    make_send(
                        sent.at[step, step_f],
                        landed.at[z, p],
                        back_send.at[at],
                        back_recv.at[z, (-step_f) % RING, number],
                        device(step_f, planes[step], core),
                    )

    def relay(step, step_f, way):
        arrive(step, step_f, "N")
        way(step, step_f, "N")
        swap(step, step_f, "N")

    def take_near(*items):
        def body():
            for step, step_f in items:
                take(step, step_f, "N")

        only("end", body)

    def relay_near(way, *items):
        def body():
            for step, step_f in items:
                relay(step, step_f, way)

        only("inner", body)

    def pass_far(kind, *steps):
        def body():
            for step in steps:
                arrive(step, 0, kind)
                (inwards if step == 1 else outwards)(step, 0, kind)
            for step in steps:
                swap(step, 0, kind)

        only("inner", body)

    def forward(step):
        for step_f, by, kind in ((3, 1, "A"), (1, 3, "B")):
            arrive(step, step_f, kind)
            around(step, step_f, kind, by)
            swap(step, step_f, kind)

    def first_halves(step):
        around(step, 0, "A", 1)
        around(step, 0, "B", 3)

    def second_halves(step):
        around(step, 0, "B", 1)
        around(step, 0, "A", 3)

    def take_pair(step):
        take(step, 3, "B")
        take(step, 1, "A")

    def take_last(step):
        take(step, 2, "A")
        take(step, 2, "B")

    def score(first, last):
        scored = jnp.dot(
            down_buf[first:last, :], head_ref[...], preferred_element_type=jnp.float32
        )
        high = scored.astype(jnp.bfloat16)
        scored_buf[first:last, :actions_count] = high
        scored_buf[first:last, actions_count:] = (
            scored - high.astype(jnp.float32)
        ).astype(jnp.bfloat16)

    tiles = hidden_units // TILE
    load_gate.wait()
    load_up.wait()
    for tile in range(tiles):
        turn(tile)
    for step_f, by, kind in ((3, 1, "a"), (1, 3, "b")):
        arrive(0, step_f, "N")
        around(0, step_f, kind, by)
        only("end", lambda: inwards(0, step_f, "N"))
        swap(0, step_f, "N")
    second_halves(0)
    pass_far("A", 1, 2)
    only("end", lambda: take(1, 0, "A"))
    load_down.wait()
    score(0, tiles // 2 * TILE)
    forward(0)
    pass_far("B", 1, 2)

    def pass_own():
        for step_f in (0, 3):
            outwards(0, step_f, "N")
            inwards(0, step_f, "N")

    only("inner", pass_own)
    only("end", lambda: take(1, 0, "B"))
    arrive(0, 2, "a")
    arrive(0, 2, "b")
    only("end", lambda: inwards(0, 2, "N"))
    swap(0, 2, "N")
    first_halves(1)
    second_halves(1)
    score(tiles // 2 * TILE, hidden_units)
    take_pair(0)
    pass_far("A", 3)
    only("end", lambda: take(2, 0, "A"))
    chunk((0, 0, "W"))
    pass_far("B", 3)
    only("end", lambda: take(2, 0, "B"))
    first_halves(2)
    relay_near(inwards, (1, 0), (1, 3))
    take_last(0)
    chunk((0, 3, "W"), (0, 1, "W"))
    forward(1)
    second_halves(2)

    def pass_more():
        relay(1, 1, inwards)
        relay(1, 2, inwards)
        inwards(0, 1, "N")
        inwards(0, 2, "N")
        relay(2, 0, outwards)
        relay(2, 3, outwards)

    only("inner", pass_more)
    take_near((1, 0), (1, 3))
    give_back((0, 0, "W"))
    chunk((0, 2, "W"), (1, 0, "F"))
    take_pair(1)
    relay_near(outwards, (3, 0), (3, 3))
    only("end", lambda: take(3, 0, "A"))
    give_back((0, 3, "W"), (0, 1, "W"))
    chunk((2, 0, "F"), (1, 0, "N"), (1, 3, "N"))
    only("end", lambda: take(3, 0, "B"))
    first_halves(3)
    forward(2)
    second_halves(3)
    give_back((0, 2, "W"), (1, 0, "F"))
    chunk((1, 3, "F"), (1, 1, "F"))
    relay_near(outwards, (3, 1), (3, 2))
    take_last(1)
    take_near((2, 0))
    take_pair(2)
    give_back((2, 0, "F"), (1, 0, "N"), (1, 3, "N"))
    chunk((1, 2, "F"), (3, 0, "F"))

    def pass_last():
        relay(2, 1, outwards)
        relay(2, 2, outwards)
        outwards(0, 1, "N")
        outwards(0, 2, "N")

    only("inner", pass_last)
    take_near((2, 3), (3, 0), (3, 3))
    forward(3)
    give_back((1, 3, "F"), (1, 1, "F"))
    chunk((2, 3, "F"), (2, 1, "F"))
    take_last(2)
    take_near((3, 1))
    give_back((1, 2, "F"), (3, 0, "F"))
    chunk((2, 0, "N"), (2, 3, "N"), (3, 0, "N"), (3, 3, "N"))
    take_pair(3)
    give_back((2, 3, "F"), (2, 1, "F"))
    chunk((2, 2, "F"))
    take_near((3, 2), (2, 1), (2, 2))
    take_last(3)
    give_back((2, 0, "N"), (2, 3, "N"), (3, 0, "N"), (3, 3, "N"))
    chunk((3, 3, "F"), (3, 1, "F"), (3, 1, "N"))
    take_near((1, 1), (1, 2))
    give_back((2, 2, "F"))
    chunk((3, 2, "F"), (3, 2, "N"), (2, 1, "N"), (2, 2, "N"))
    give_back((3, 3, "F"), (3, 1, "F"), (3, 1, "N"))
    chunk((1, 1, "N"), (1, 2, "N"))
    give_back((3, 2, "F"), (3, 2, "N"), (2, 1, "N"), (2, 2, "N"))
    give_back((1, 1, "N"), (1, 2, "N"))

    trace_row = trace_ref[...].astype(jnp.float32) / 1024.0
    trace_col = column(trace_row)
    reward_col = column(rewards_ref[...].astype(jnp.float32) * 0.25)
    action_col = column(actions_ref[...].astype(jnp.float32))
    log_row = jnp.log(DISCOUNT * trace_row)
    log_col = column(log_row)
    sums_row = jnp.sum(jnp.where(first_axis <= second_axis, log_col, 0.0), axis=0, keepdims=True)
    sums_col = jnp.sum(jnp.where(second_axis <= first_axis, log_row, 0.0), axis=1, keepdims=True)
    weight = jnp.where(
        first_axis >= second_axis, jnp.exp(jnp.minimum(sums_col - sums_row, 0.0)), 0.0
    )
    action_axis = lax.broadcasted_iota(jnp.int32, (rows, actions_count), 1).astype(jnp.float32)
    chosen = action_axis == action_col

    for step in range(RING):
        for step_f in range(RING):
            if (step, step_f) != (0, 0):
                for number, landed in enumerate((near_landed, far_landed)):
                    await_in(
                        landed.at[planes[step], (p + step_f) % RING],
                        back_recv.at[planes[step], step_f, number],
                    )
    blended = []
    for landed, first in ((near_landed, 0), (far_landed, near)):
        height = landed.shape[2]
        at = pl.ds(pl.multiple_of(first + core * height, 16), height)
        total = jnp.zeros((height, actions_count), jnp.float32)
        for expert in range(RING):
            part_sum = jnp.zeros((height, actions_count), jnp.float32)
            for place in range(RING):
                part_sum = part_sum + landed[expert, place].astype(jnp.float32)
            total = total + share_buf[expert, at, :] * part_sum
        blended.append(total)
    halves[core] = jnp.concatenate(blended, axis=0)
    make_send(
        halves.at[core], halves.at[core], pair_send.at[1], pair_recv.at[1], device(0, z, other)
    )
    await_in(halves.at[other], pair_recv.at[1])
    values = jnp.concatenate(
        [
            halves[0, :near_half],
            halves[1, :near_half],
            halves[0, near_half:],
            halves[1, near_half:],
        ],
        axis=0,
    )
    values_ref[...] = values
    greedy = jnp.max(values, axis=1, keepdims=True)
    taken = jnp.sum(jnp.where(chosen, values, 0.0), axis=1, keepdims=True)
    ahead_row = row_of(greedy - trace_col * taken)
    ahead = jnp.sum(
        jnp.where(second_axis == first_axis + 1, ahead_row, 0.0), axis=1, keepdims=True
    )
    driver = reward_col + DISCOUNT * ahead
    targets_ref[...] = jnp.sum(weight * driver, axis=0, keepdims=True)
    for which in (None, "end", "inner"):
        makes = [make for owner, make in sends if owner == which]

        def finish(makes=makes):
            for make in makes:
                make().wait_send()

        if which is None:
            finish()
        else:
            pl.when(at_end if which == "end" else inner)(finish)


def per_device(
    tokens,
    norm_gain,
    expert_ids,
    gate_codes,
    gate_weights,
    up_weights,
    down_weights,
    value_head,
    actions,
    rewards,
    trace_codes,
):
    rows, wide = tokens.shape
    hidden_units, features = gate_weights.shape[1:]
    actions_count = value_head.shape[1]
    near_half = rows // 8
    far_half = rows // 2 - near_half
    most = 2 * rows
    blocks = (RING, RING)
    vmem = pl.BlockSpec(memory_space=pltpu.VMEM)
    hbm = pl.BlockSpec(memory_space=pltpu.HBM)
    dma = pltpu.SemaphoreType.DMA
    values, targets = pl.pallas_call(
        critic_kernel,
        out_shape=(
            jax.ShapeDtypeStruct((rows, actions_count), jnp.float32),
            jax.ShapeDtypeStruct((1, rows), jnp.float32),
        ),
        in_specs=[hbm, vmem, vmem, vmem, hbm, hbm, hbm, vmem, vmem, vmem, vmem],
        out_specs=(vmem, vmem),
        scratch_shapes=[
            pltpu.VMEM((rows, wide), jnp.bfloat16),
            pltpu.VMEM((2, *blocks, rows, wide), jnp.bfloat16),
            pltpu.VMEM((hidden_units, features), jnp.bfloat16),
            pltpu.VMEM((hidden_units, features), jnp.bfloat16),
            pltpu.VMEM((hidden_units, features), jnp.bfloat16),
            pltpu.VMEM((features, 2 * hidden_units), jnp.bfloat16),
            pltpu.VMEM((hidden_units, 2 * actions_count), jnp.bfloat16),
            pltpu.VMEM((most, hidden_units), jnp.bfloat16),
            pltpu.VMEM((2, 1, rows), jnp.float32),
            pltpu.VMEM((*blocks, 1, rows), jnp.float32),
            pltpu.VMEM((*blocks, rows, TILE), jnp.float32),
            pltpu.VMEM((*blocks, 2, near_half, actions_count), jnp.float32),
            pltpu.VMEM((*blocks, 2, far_half, actions_count), jnp.float32),
            pltpu.VMEM((*blocks, near_half, actions_count), jnp.float32),
            pltpu.VMEM((*blocks, far_half, actions_count), jnp.float32),
            pltpu.VMEM((*blocks, near_half, actions_count), jnp.bfloat16),
            pltpu.VMEM((*blocks, far_half, actions_count), jnp.bfloat16),
            pltpu.VMEM((*blocks, near_half, actions_count), jnp.bfloat16),
            pltpu.VMEM((*blocks, far_half, actions_count), jnp.bfloat16),
            pltpu.VMEM((RING, rows, actions_count), jnp.float32),
            pltpu.VMEM((2, rows // 2, actions_count), jnp.float32),
            dma((4,)),
            dma((2,)),
            dma((2,)),
            dma((2, 64)),
            dma((*blocks, 4)),
            dma((*blocks, 4)),
            dma((*blocks, 4)),
            dma(blocks),
            dma((32,)),
            dma((32,)),
            dma((32,)),
            dma((*blocks, 2)),
        ],
        compiler_params=pltpu.CompilerParams(
            collective_id=0, has_side_effects=True, vmem_limit_bytes=60 * 1024 * 1024
        ),
    )(
        tokens,
        norm_gain.reshape(1, -1),
        expert_ids.T,
        gate_codes.T,
        gate_weights,
        up_weights,
        down_weights,
        value_head,
        actions.reshape(1, -1),
        rewards.reshape(1, -1),
        trace_codes.reshape(1, -1),
    )
    return values, targets.reshape(-1)


def solution(mesh):
    in_specs = (
        P(("dp", "expert"), "tensor"),
        P(),
        P(("dp", "expert"), None),
        P(("dp", "expert"), None),
        P("expert", ("dp", "tensor"), None),
        P("expert", ("dp", "tensor"), None),
        P("expert", ("dp", "tensor"), None),
        P(),
        P(("dp", "expert")),
        P(("dp", "expert")),
        P(("dp", "expert")),
    )
    out_specs = (P(("dp", "expert"), None), P(("dp", "expert")))
    shape = mesh.shape
    rings = shape["dp"] == RING and shape["expert"] == RING and shape["tensor"] == 2
    body = per_device if rings else per_device_plain
    return jax.shard_map(
        body, mesh=mesh, in_specs=in_specs, out_specs=out_specs, check_vma=False
    )
```

time: 76.6 us -> 61.7 us (0.81)
  Pallas kernels: 71.8 us -> 56.9 us
    pallas_call x1, Pallas kernels: 71.8 us -> 56.9 us  [per_device(): pl.pallas_call(critic_kernel, out_shape=(jax.ShapeDtypeStruct((rows, acti...]
where the time goes in v1:
time: 61.7 us; the launch traced here: 61.5 us
  Pallas kernels  56.9 us (92%)
  local copies, waits for them, and re-layouts  3.88 us (6%)
  between operations  0.64 us (1%)
    pallas_call x1, Pallas kernels, per_device(): pl.pallas_call(critic_kernel, out_shape=(jax.ShapeDtypeStruct((rows, acti...  56.9 us
    unnamed x2, local copies, waits for them, and re-layouts  2.59 us
    reshape x1, local copies, waits for them, and re-layouts, per_device(): norm_gain.reshape(1, -1)  1.29 us

profile of v1, /device:TPU:1, one launch (start us, length us, event | category | flops | bytes accessed | tf_op | source)
XLA Modules:
  0.0 61.5 jit_solution(13301675962436933863)
XLA Ops:
  0.6 1.3 %reshape.19.gain_ref = bf16[1,2048]{1,0:T(2,128)(2,1)} reshape(bf16[2048]{0:T(1024)(128)(2,1)} %param.12) | data formatting | bytes 8192 | tf_op jit(solution)/shard_map/reshape | solution.py:783
  1.9 56.9 %shard_map.122 = (f32[128,128]{1,0:T(8,128)}, f32[1,128]{1,0:T(1,128)}) custom-call(bf16[128,1024]{1,0:T(8,128)(2,1)} %tokens_ref.1, bf16[1,2048]{1,0:T(2,128)(2,1)} %reshape.19.gain_ref, s32[2,128]{1,0:T(2,128)} %bitcast.6, s32[2,128]{1,0:T(2,128)} %bitcast.7, bf16[1,896,2048]{2,1,0:T(8,128)(2,1)} %gate_ref.1, bf16[1,896,2048]{2,1,0:T(8,128)(2,1)} %up_ref.1, ...), custom_call_target="tpu_custom_call" | custom-call | tf_op jit(solution)/shard_map/pallas_call | solution.py:735
  58.9 1.5 %copy.15 = f32[128,128]{1,0:T(8,128)} copy(f32[128,128]{1,0:T(8,128)} %get-tuple-element.8) | data formatting | bytes 131072
  60.3 1.1 %copy.16 = f32[128]{0:T(128)} copy(f32[128]{0:T(128)} %bitcast.11) | data formatting | bytes 1024

commit v2 on v1

v2 whole, which is shorter than its diff:
```python
import jax
import jax.numpy as jnp
from jax import lax
from jax.experimental import pallas as pl
from jax.experimental.pallas import tpu as pltpu
from jax.sharding import PartitionSpec as P

TOP = 2
STEPS = 128


DISCOUNT = 0.99
EPSILON = 1e-05


def expert_rows(row_block, gate_matrix, lift_matrix, down_matrix):
    gate_value = lax.dot_general(
        row_block, gate_matrix, (((1,), (1,)), ((), ())), preferred_element_type=jnp.float32
    )
    lift_value = lax.dot_general(
        row_block, lift_matrix, (((1,), (1,)), ((), ())), preferred_element_type=jnp.float32
    )
    hidden = (jax.nn.silu(gate_value) * lift_value).astype(jnp.bfloat16)
    return jnp.dot(hidden, down_matrix, preferred_element_type=jnp.float32)


def retrace(action_values, actions, rewards, trace_codes):
    greedy = jnp.max(action_values, axis=1)
    picked = (
        actions[:, None] == jnp.arange(action_values.shape[1], dtype=jnp.int32)[None, :]
    ).astype(jnp.float32)
    taken = jnp.sum(action_values * picked, axis=1)
    trace = trace_codes.astype(jnp.float32) / 1024.0
    reward = rewards.astype(jnp.float32) * 0.25
    greedy = greedy.reshape(-1, STEPS)
    taken = taken.reshape(-1, STEPS)
    trace = trace.reshape(-1, STEPS)
    reward = reward.reshape(-1, STEPS)
    padding = jnp.zeros_like(greedy[:, :1])
    greedy_next = jnp.concatenate([greedy[:, 1:], padding], axis=1)
    taken_next = jnp.concatenate([taken[:, 1:], padding], axis=1)
    trace_next = jnp.concatenate([trace[:, 1:], padding], axis=1)
    driver = reward + DISCOUNT * (greedy_next - trace_next * taken_next)
    log_sums = jnp.cumsum(jnp.log(DISCOUNT * trace), axis=1)
    spans = log_sums[:, None, :] - log_sums[:, :, None]
    upper_mask = (
        jnp.arange(STEPS, dtype=jnp.int32)[None, :] >= jnp.arange(STEPS, dtype=jnp.int32)[:, None]
    )
    weight = jnp.where(upper_mask[None, :, :], jnp.exp(jnp.minimum(spans, 0.0)), 0.0)
    target = jnp.einsum("nts,ns->nt", weight, driver, precision=lax.Precision.HIGHEST)
    return target.reshape(-1)


def per_device_plain(
    tokens,
    norm_gain,
    expert_ids,
    gate_codes,
    gate_weights,
    up_weights,
    down_weights,
    value_head,
    actions,
    rewards,
    trace_codes,
):
    mesh_rows = ("dp", "expert")
    expert = lax.axis_index("expert")
    codes = gate_codes.astype(jnp.float32)
    gate_share = codes / jnp.sum(codes, axis=1, keepdims=True)
    experts = jnp.arange(lax.axis_size("expert"), dtype=jnp.int32)
    share = jnp.sum(
        jnp.where(expert_ids[:, :, None] == experts[None, None, :], gate_share[:, :, None], 0.0),
        axis=1,
    )
    every_share = lax.all_gather(share, mesh_rows, axis=0, tiled=True)
    own_share = lax.dynamic_slice_in_dim(every_share, expert, 1, axis=1)
    full = lax.all_gather(tokens, "tensor", axis=1, tiled=True)
    widened = full.astype(jnp.float32)
    scaling = lax.rsqrt(jnp.mean(widened * widened, axis=1, keepdims=True) + EPSILON)
    normed = (widened * scaling * norm_gain.astype(jnp.float32)[None, :]).astype(jnp.bfloat16)
    gathered = lax.all_gather(normed, mesh_rows, axis=0, tiled=True)
    scored = jnp.dot(down_weights[0], value_head, preferred_element_type=jnp.float32)
    high = scored.astype(jnp.bfloat16)
    low = (scored - high.astype(jnp.float32)).astype(jnp.bfloat16)
    both = jnp.concatenate([high, low], axis=1)
    wide = expert_rows(gathered, gate_weights[0], up_weights[0], both)
    actions_count = value_head.shape[1]
    partial_values = (wide[:, :actions_count] + wide[:, actions_count:]) * own_share
    partial_values = lax.psum_scatter(partial_values, mesh_rows, scatter_dimension=0, tiled=True)
    action_values = lax.psum(partial_values, "tensor")
    retrace_targets = retrace(action_values, actions, rewards, trace_codes)
    return (action_values, retrace_targets)


RING = 4
MESH = pl.DeviceIdType.MESH
TILE = 128
COMPUTE = True
CHUNKS = (
    ((0, 0, "W"),),
    ((1, 0, "F"),),
    ((0, 3, "W"), (0, 1, "W")),
    ((0, 2, "W"), (2, 0, "F")),
    ((1, 3, "F"), (1, 1, "F"), (1, 0, "N"), (1, 3, "N")),
    ((1, 2, "F"), (3, 0, "F"), (2, 0, "N")),
    ((2, 3, "F"), (2, 1, "F"), (2, 3, "N")),
    ((2, 2, "F"), (3, 0, "N"), (3, 3, "N"), (3, 1, "N")),
    ((3, 3, "F"), (3, 1, "F"), (3, 2, "N")),
    ((3, 2, "F"), (2, 1, "N"), (2, 2, "N")),
    ((1, 1, "N"), (1, 2, "N")),
)
GROUPS = ((0, 1, 2), (3, 4), (5, 6), (7, 8), (9,), (10,))
STRAIGHT = (4, 5)


def gray(place):
    return place + (place // 2) * (1 - 2 * (place % 2))


def critic_kernel(
    tokens_ref,
    gain_hbm,
    ids_hbm,
    codes_hbm,
    gate_ref,
    up_ref,
    down_ref,
    head_hbm,
    actions_hbm,
    rewards_hbm,
    trace_hbm,
    outcome_ref,
    raw,
    gain_ref,
    gain_rows,
    ids_ref,
    codes_ref,
    head_ref,
    actions_ref,
    rewards_ref,
    trace_ref,
    held,
    gate_buf,
    up_buf,
    down_buf,
    turned,
    scored_buf,
    hidden_buf,
    squares,
    partial,
    given,
    sent,
    near_landed,
    far_landed,
    share_buf,
    halves,
    load_sems,
    send_sem,
    pair_recv,
    move_recv,
    swap_recv,
    give_recv,
    back_recv,
):
    dp = lax.axis_index("dp")
    z = lax.axis_index("expert")
    core = lax.axis_index("tensor")
    other = 1 - core
    p = gray(dp)
    rows, wide = tokens_ref.shape
    hidden_units = gate_ref.shape[1]
    actions_count = head_hbm.shape[1]
    near = rows // 4
    near_half = near // 2
    far_half = (rows - near) // 2
    spans = {
        "W": (0, rows),
        "N": (0, near),
        "F": (near, rows - near),
        "a": (0, near_half),
        "b": (near_half, near_half),
        "A": (near, far_half),
        "B": (near + far_half, far_half),
    }
    inward = jnp.where(z < RING // 2, 1, -1)
    at_end = jnp.logical_or(z == 0, z == RING - 1)
    inner = jnp.logical_not(at_end)
    planes = tuple(z + (step & 1) * (1 - 2 * (z % 2)) + (step & 2) * (1 - (z // 2) * 2) for step in range(RING))

    def device(step_p, plane, which):
        return (gray((p + step_p) % RING), plane, which)

    load_token = pltpu.make_async_copy(tokens_ref, raw, load_sems.at[0])
    load_gate = pltpu.make_async_copy(gate_ref.at[0], gate_buf, load_sems.at[1])
    load_up = pltpu.make_async_copy(up_ref.at[0], up_buf, load_sems.at[2])
    load_down = pltpu.make_async_copy(down_ref.at[0], down_buf, load_sems.at[3])
    load_head = pltpu.make_async_copy(head_hbm, head_ref, load_sems.at[4])
    load_gain = pltpu.make_async_copy(gain_hbm, gain_ref, load_sems.at[5])
    small = [
        pltpu.make_async_copy(source, target, load_sems.at[6 + number])
        for number, (source, target) in enumerate(
            (
                (ids_hbm, ids_ref),
                (codes_hbm, codes_ref),
                (actions_hbm, actions_ref),
                (rewards_hbm, rewards_ref),
                (trace_hbm, trace_ref),
            )
        )
    ]
    load_token.start()
    load_gain.start()
    load_gate.start()
    load_up.start()
    for load in small:
        load.start()
    load_down.start()
    load_head.start()

    barrier = pltpu.get_barrier_semaphore()

    def greet(to):
        pl.semaphore_signal(barrier, inc=1, device_id=to, device_id_type=MESH)

    greet(device(0, z, other))
    greet(device(1, z, core))
    greet(device(3, z, core))
    greet(device(0, z + inward, core))
    pl.when(inner)(lambda: greet(device(0, z - inward, core)))

    sends = []
    group = [None]
    held_back = []

    def make_send(source, target, recv_sem, to):
        def make():
            return pltpu.make_async_remote_copy(
                src_ref=source,
                dst_ref=target,
                send_sem=send_sem.at[0],
                recv_sem=recv_sem,
                device_id=to,
                device_id_type=MESH,
            )

        sends.append((group[0], make))
        act(lambda: make().start())

    def await_in(target, recv_sem):
        sibling = device(0, z, other)
        act(
            lambda: pltpu.make_async_remote_copy(
                src_ref=target,
                dst_ref=target,
                send_sem=recv_sem,
                recv_sem=recv_sem,
                device_id=sibling,
                device_id_type=MESH,
            ).wait_recv()
        )

    def act(step):
        if group[0] is None:
            step()
        else:
            held_back.append(step)

    def only(which, body):
        group[0] = which
        body()
        group[0] = None
        steps = list(held_back)
        held_back.clear()

        def run():
            for step in steps:
                step()

        pl.when(at_end if which == "end" else inner)(run)

    def piece(which, step, step_f, kind):
        first, count = spans[kind]
        return held.at[which, planes[step], (p + step_f) % RING, pl.ds(first, count)]

    def moved(step, step_f, kind):
        if kind in "Nab":
            return move_recv.at[planes[step], 5 + step_f]
        slots = {"A": (0, 3, 4, 2), "B": (1, 2, 4, 3)}[kind]
        return move_recv.at[planes[step], slots[step_f]]

    def move(step, step_f, kind, by, plane):
        here = piece(core, step, step_f, kind)
        there = moved(step, (step_f - by) % RING, kind)
        make_send(here, here, there, device(by, plane, core))

    def around(step, step_f, kind, by):
        move(step, step_f, kind, by, z)

    def inwards(step, step_f, kind):
        move(step, step_f, kind, 0, z + inward)

    def outwards(step, step_f, kind):
        move(step, step_f, kind, 0, z - inward)

    def arrive(step, step_f, kind):
        await_in(piece(core, step, step_f, kind), moved(step, step_f, kind))

    def arrive_both(step, step_f, kind):
        await_in(piece(core, step, step_f, "F"), moved(step, step_f, kind))

    def chunk_of(step, step_f, kind):
        wanted = "N" if kind == "N" else "F"
        for number, items in enumerate(CHUNKS):
            if (step, step_f, wanted) in items or (step, step_f, "W") in items:
                return number
        raise KeyError(kind)

    def swap(step, step_f, kind):
        here = piece(core, step, step_f, kind)
        make_send(here, here, swap_recv.at[chunk_of(step, step_f, kind)], device(0, z, other))

    def take(step, step_f, kind):
        arrive(step, step_f, kind)
        swap(step, step_f, kind)

    first_axis = lax.broadcasted_iota(jnp.int32, (rows, rows), 0)
    second_axis = lax.broadcasted_iota(jnp.int32, (rows, rows), 1)
    same = first_axis == second_axis

    def column(row):
        return jnp.sum(jnp.where(same, row, 0.0), axis=1, keepdims=True)

    def row_of(col):
        return jnp.sum(jnp.where(same, col, 0.0), axis=0, keepdims=True)

    load_token.wait()
    widened = raw[...].astype(jnp.float32)
    squares[core] = jnp.broadcast_to(
        jnp.sum(widened * widened, axis=1, keepdims=True), (rows, TILE)
    )
    load_gain.wait()
    gain_rows[...] = gain_ref[...].astype(jnp.float32)
    pl.semaphore_wait(barrier, jnp.where(at_end, 4, 5))
    make_send(squares.at[core], squares.at[core], pair_recv.at[0], device(0, z, other))
    await_in(squares.at[other], pair_recv.at[0])
    total = squares[0] + squares[1]
    scaling = lax.rsqrt(total / (2 * wide) + EPSILON)
    cuts = wide // TILE
    for cut in range(cuts):
        gain = gain_rows[pl.ds(core * cuts + cut, 1), :]
        at = cut * TILE
        held[core, z, p, :, at : at + TILE] = (widened[:, at : at + TILE] * scaling * gain).astype(
            jnp.bfloat16
        )

    around(0, 0, "N", 1)
    around(0, 0, "N", 3)
    inwards(0, 0, "A")
    only("inner", lambda: outwards(0, 0, "A"))
    swap(0, 0, "W")

    for load in small:
        load.wait()
    codes = codes_ref[...].astype(jnp.float32)
    gate_share = codes / jnp.sum(codes, axis=0, keepdims=True)
    ids = ids_ref[...]
    for expert in range(RING):
        share = jnp.sum(jnp.where(ids == expert, gate_share, 0.0), axis=0, keepdims=True)
        share_buf[expert] = jnp.broadcast_to(column(share), (rows, actions_count))

    around(0, 0, "A", 1)
    around(0, 0, "B", 3)
    inwards(0, 0, "B")
    only("end", lambda: inwards(0, 0, "N"))
    only("inner", lambda: outwards(0, 0, "B"))

    def turn(tile):
        at = tile * TILE
        turned[:, 2 * at : 2 * at + TILE] = gate_buf[at : at + TILE, :].T
        turned[:, 2 * at + TILE : 2 * at + 2 * TILE] = up_buf[at : at + TILE, :].T

    def height(kind):
        return spans[kind][1]

    def halves_of(kind):
        if kind in "WN":
            yield 0, near_half
        if kind in "WF":
            yield 1, far_half

    def chunk(number):
        base = sum(
            height(kind)
            for members in GROUPS
            if number in members
            for before in members
            if before < number
            for _, _, kind in CHUNKS[before]
        )
        parts = [
            (planes[step], (p + step_f) % RING, *spans[kind])
            for step, step_f, kind in CHUNKS[number]
        ]
        count = sum(part[3] for part in parts)
        await_in(gate_buf.at[pl.ds(0, count // 2)], swap_recv.at[number])
        for tile in range(hidden_units // TILE if COMPUTE else 0):
            at = tile * TILE
            lhs = jnp.concatenate(
                [
                    jnp.concatenate(
                        [
                            held[which, plane, place, first : first + size]
                            for plane, place, first, size in parts
                        ],
                        axis=0,
                    )
                    for which in range(2)
                ],
                axis=1,
            )
            both = jnp.dot(
                lhs, turned[:, 2 * at : 2 * at + 2 * TILE], preferred_element_type=jnp.float32
            )
            hidden_buf[base : base + count, at : at + TILE] = (
                jax.nn.silu(both[:, :TILE]) * both[:, TILE:]
            ).astype(jnp.bfloat16)

    def items_of(number):
        return [item for member in GROUPS[number] for item in CHUNKS[member]]

    def results(number):
        items = items_of(number)
        count = sum(height(kind) for _, _, kind in items)
        result = jnp.dot(
            hidden_buf[:count, :], scored_buf[...], preferred_element_type=jnp.float32
        )
        result = result[:, :actions_count] + result[:, actions_count:]
        offset, target = 0, 0
        for _, _, kind in items:
            for _, half in halves_of(kind):
                for which in range(2):
                    rows_here = result[offset + which * half : offset + (which + 1) * half]
                    if number in STRAIGHT:
                        sent[number, which, target : target + half] = rows_here.astype(
                            jnp.bfloat16
                        )
                    else:
                        partial[number, which, target : target + half] = rows_here
                offset += 2 * half
                target += half
        if number in STRAIGHT:
            give_back(number)
        else:
            make_send(
                partial.at[number, other, pl.ds(0, target)],
                given.at[number, pl.ds(0, target)],
                give_recv.at[number],
                device(0, z, other),
            )

    def give_back(number):
        items = items_of(number)
        straight = number in STRAIGHT
        count = sum(height(kind) for _, _, kind in items) // 2
        if not straight:
            await_in(given.at[number, pl.ds(0, count)], give_recv.at[number])
            sent[number, 0, :count] = (
                partial[number, core, :count] + given[number, :count]
            ).astype(jnp.bfloat16)
        target = 0
        for step, step_f, kind in items:
            for part, half in halves_of(kind):
                landed = (near_landed, far_landed)[part]
                for which in range(2 if straight else 1):
                    here = sent.at[number, which, pl.ds(target, half)]
                    if (step, step_f) == (0, 0):
                        landed[core, RING * z + p] = sent[number, 0, target : target + half]
                    else:
                        make_send(
                            here,
                            landed.at[core, RING * z + p],
                            back_recv.at[2 * straight + part],
                            device(step_f, planes[step], which if straight else core),
                        )
                target += half

    def relay(step, step_f, way):
        arrive(step, step_f, "N")
        way(step, step_f, "N")
        swap(step, step_f, "N")

    def take_near(*items):
        def body():
            for step, step_f in items:
                take(step, step_f, "N")

        only("end", body)

    def relay_near(way, *items):
        def body():
            for step, step_f in items:
                relay(step, step_f, way)

        only("inner", body)

    def pass_far(kind, *steps):
        def body():
            for step in steps:
                arrive(step, 0, kind)
                (inwards if step == 1 else outwards)(step, 0, kind)
            for step in steps:
                swap(step, 0, kind)

        only("inner", body)

    def forward(step):
        arrive_both(step, 3, "A")
        for step_f, by, kind in ((3, 1, "A"), (1, 3, "B")):
            around(step, step_f, kind, by)
            swap(step, step_f, kind)

    def first_halves(step):
        around(step, 0, "A", 1)
        around(step, 0, "B", 3)

    def second_halves(step):
        around(step, 0, "B", 1)
        around(step, 0, "A", 3)

    def take_pair(step):
        arrive_both(step, 3, "B")
        swap(step, 3, "B")
        swap(step, 1, "A")

    def take_last(step):
        arrive_both(step, 2, "A")
        swap(step, 2, "F")

    def score(first, last):
        scored = jnp.dot(
            down_buf[first:last, :], head_ref[...], preferred_element_type=jnp.float32
        )
        high = scored.astype(jnp.bfloat16)
        scored_buf[first:last, :actions_count] = high
        scored_buf[first:last, actions_count:] = (
            scored - high.astype(jnp.float32)
        ).astype(jnp.bfloat16)

    tiles = hidden_units // TILE
    load_gate.wait()
    load_up.wait()
    for tile in range(tiles):
        turn(tile)
    for step_f, by, kind in ((3, 1, "a"), (1, 3, "b")):
        arrive(0, step_f, "N")
        around(0, step_f, kind, by)
        only("end", lambda: inwards(0, step_f, "N"))
        swap(0, step_f, "N")
    second_halves(0)
    pass_far("A", 1, 3)
    only("end", lambda: take(1, 0, "A"))
    chunk(0)
    forward(0)
    pass_far("B", 1, 3)

    def pass_own():
        for step_f in (0, 3):
            outwards(0, step_f, "N")
            inwards(0, step_f, "N")

    only("inner", pass_own)
    only("end", lambda: take(1, 0, "B"))
    load_down.wait()
    load_head.wait()
    score(0, tiles // 2 * TILE)
    arrive(0, 2, "N")
    only("end", lambda: inwards(0, 2, "N"))
    swap(0, 2, "N")
    first_halves(1)
    second_halves(1)
    score(tiles // 2 * TILE, hidden_units)
    take_pair(0)
    pass_far("A", 2)
    only("end", lambda: take(2, 0, "A"))
    chunk(1)
    take_last(0)
    pass_far("B", 2)
    only("end", lambda: take(2, 0, "B"))
    first_halves(2)
    relay_near(inwards, (1, 0), (1, 3))
    chunk(2)
    forward(1)
    second_halves(2)

    def pass_more():
        relay(1, 1, inwards)
        relay(1, 2, inwards)
        inwards(0, 1, "N")
        inwards(0, 2, "N")
        relay(3, 0, outwards)
        relay(3, 3, outwards)

    only("inner", pass_more)
    take_near((1, 0), (1, 3))
    results(0)
    chunk(3)
    take_pair(1)
    relay_near(outwards, (2, 0), (2, 3))
    only("end", lambda: take(3, 0, "A"))
    give_back(0)
    only("end", lambda: take(3, 0, "B"))
    first_halves(3)
    forward(2)
    second_halves(3)
    chunk(4)
    relay_near(outwards, (2, 1), (2, 2))
    take_last(1)
    take_near((2, 0))
    results(1)
    take_pair(2)
    take_near((2, 3))

    def pass_last():
        relay(3, 1, outwards)
        relay(3, 2, outwards)
        outwards(0, 1, "N")
        outwards(0, 2, "N")

    only("inner", pass_last)
    chunk(5)
    give_back(1)
    forward(3)
    take_near((3, 0), (3, 3), (3, 1))
    chunk(6)
    take_last(2)
    results(2)
    take_pair(3)
    take_near((3, 2))
    chunk(7)
    give_back(2)
    take_last(3)
    take_near((2, 1), (2, 2))
    chunk(8)
    take_near((1, 1), (1, 2))
    results(3)
    chunk(9)
    results(4)
    give_back(3)
    chunk(10)
    results(5)

    trace_row = trace_ref[...].astype(jnp.float32) / 1024.0
    trace_col = column(trace_row)
    reward_col = column(rewards_ref[...].astype(jnp.float32) * 0.25)
    action_col = column(actions_ref[...].astype(jnp.float32))
    log_row = jnp.log(DISCOUNT * trace_row)
    log_col = column(log_row)
    sums_row = jnp.sum(jnp.where(first_axis <= second_axis, log_col, 0.0), axis=0, keepdims=True)
    sums_col = jnp.sum(jnp.where(second_axis <= first_axis, log_row, 0.0), axis=1, keepdims=True)
    weight = jnp.where(
        first_axis >= second_axis, jnp.exp(jnp.minimum(sums_col - sums_row, 0.0)), 0.0
    )
    action_axis = lax.broadcasted_iota(jnp.int32, (rows, actions_count), 1).astype(jnp.float32)
    chosen = action_axis == action_col

    straight = [
        (step, (-step_f) % RING, part)
        for number in STRAIGHT
        for step, step_f, kind in items_of(number)
        for part, _ in halves_of(kind)
    ]
    for part, landed in enumerate((near_landed, far_landed)):
        direct = sum(item[2] == part for item in straight)
        usual = RING * RING - 1 - direct
        await_in(landed.at[core, pl.ds(0, usual)], back_recv.at[part])
        await_in(landed.at[core, pl.ds(0, 2 * direct)], back_recv.at[2 + part])
    blended = []
    for part, (landed, first) in enumerate(((near_landed, 0), (far_landed, near))):
        size = landed.shape[2]
        at = pl.ds(pl.multiple_of(first + core * size, 16), size)
        total = jnp.zeros((size, actions_count), jnp.float32)
        for step in range(RING):
            part_sum = jnp.zeros((size, actions_count), jnp.float32)
            for step_f in range(RING):
                block = RING * planes[step] + (p + step_f) % RING
                if (step, step_f, part) in straight:
                    part_sum = part_sum + landed[other, block].astype(jnp.float32)
                part_sum = part_sum + landed[core, block].astype(jnp.float32)
            total = total + share_buf[planes[step], at, :] * part_sum
        blended.append(total)
    halves[core] = jnp.concatenate(blended, axis=0)
    make_send(halves.at[core], halves.at[core], pair_recv.at[1], device(0, z, other))
    await_in(halves.at[other], pair_recv.at[1])
    values = jnp.concatenate(
        [
            halves[0, :near_half],
            halves[1, :near_half],
            halves[0, near_half:],
            halves[1, near_half:],
        ],
        axis=0,
    )
    outcome_ref[:rows, :] = values
    greedy = jnp.max(values, axis=1, keepdims=True)
    taken = jnp.sum(jnp.where(chosen, values, 0.0), axis=1, keepdims=True)
    ahead_row = row_of(greedy - trace_col * taken)
    ahead = jnp.sum(
        jnp.where(second_axis == first_axis + 1, ahead_row, 0.0), axis=1, keepdims=True
    )
    driver = reward_col + DISCOUNT * ahead
    targets = jnp.sum(weight * driver, axis=0, keepdims=True)
    outcome_ref[rows:, :] = jnp.broadcast_to(targets, (outcome_ref.shape[0] - rows, rows))
    for which in (None, "end", "inner"):
        makes = [make for owner, make in sends if owner == which]

        def finish(makes=makes):
            for make in makes:
                make().wait_send()

        if which is None:
            finish()
        else:
            pl.when(at_end if which == "end" else inner)(finish)


def per_device(
    tokens,
    norm_gain,
    expert_ids,
    gate_codes,
    gate_weights,
    up_weights,
    down_weights,
    value_head,
    actions,
    rewards,
    trace_codes,
):
    rows, wide = tokens.shape
    hidden_units, features = gate_weights.shape[1:]
    actions_count = value_head.shape[1]
    near_half = rows // 8
    far_half = rows // 2 - near_half
    most = 4 * rows
    groups = len(GROUPS)
    blocks = (RING, RING)
    vmem = pl.BlockSpec(memory_space=pltpu.VMEM)
    hbm = pl.BlockSpec(memory_space=pltpu.HBM)
    dma = pltpu.SemaphoreType.DMA
    outcome = pl.pallas_call(
        critic_kernel,
        out_shape=jax.ShapeDtypeStruct((rows + 8, actions_count), jnp.float32),
        in_specs=[hbm] * 11,
        out_specs=vmem,
        scratch_shapes=[
            pltpu.VMEM((rows, wide), jnp.bfloat16),
            pltpu.VMEM((features // TILE, TILE), jnp.bfloat16),
            pltpu.VMEM((features // TILE, TILE), jnp.float32),
            pltpu.VMEM((2, rows), jnp.int32),
            pltpu.VMEM((2, rows), jnp.int32),
            pltpu.VMEM((features, actions_count), jnp.bfloat16),
            pltpu.VMEM((1, rows), jnp.int32),
            pltpu.VMEM((1, rows), jnp.int32),
            pltpu.VMEM((1, rows), jnp.int32),
            pltpu.VMEM((2, *blocks, rows, wide), jnp.bfloat16),
            pltpu.VMEM((hidden_units, features), jnp.bfloat16),
            pltpu.VMEM((hidden_units, features), jnp.bfloat16),
            pltpu.VMEM((hidden_units, features), jnp.bfloat16),
            pltpu.VMEM((features, 2 * hidden_units), jnp.bfloat16),
            pltpu.VMEM((hidden_units, 2 * actions_count), jnp.bfloat16),
            pltpu.VMEM((most, hidden_units), jnp.bfloat16),
            pltpu.VMEM((2, rows, TILE), jnp.float32),
            pltpu.VMEM((groups, 2, most // 2, actions_count), jnp.float32),
            pltpu.VMEM((groups, most // 2, actions_count), jnp.float32),
            pltpu.VMEM((groups, 2, most // 2, actions_count), jnp.bfloat16),
            pltpu.VMEM((2, RING * RING, near_half, actions_count), jnp.bfloat16),
            pltpu.VMEM((2, RING * RING, far_half, actions_count), jnp.bfloat16),
            pltpu.VMEM((RING, rows, actions_count), jnp.float32),
            pltpu.VMEM((2, rows // 2, actions_count), jnp.float32),
            dma((11,)),
            dma((1,)),
            dma((2,)),
            dma((RING, 9)),
            dma((len(CHUNKS),)),
            dma((groups,)),
            dma((4,)),
        ],
        compiler_params=pltpu.CompilerParams(
            collective_id=0, has_side_effects=True, vmem_limit_bytes=60 * 1024 * 1024
        ),
    )(
        tokens,
        norm_gain.reshape(-1, TILE),
        expert_ids.T,
        gate_codes.T,
        gate_weights,
        up_weights,
        down_weights,
        value_head,
        actions.reshape(1, -1),
        rewards.reshape(1, -1),
        trace_codes.reshape(1, -1),
    )
    return outcome[:rows], outcome[rows]


def solution(mesh):
    in_specs = (
        P(("dp", "expert"), "tensor"),
        P(),
        P(("dp", "expert"), None),
        P(("dp", "expert"), None),
        P("expert", ("dp", "tensor"), None),
        P("expert", ("dp", "tensor"), None),
        P("expert", ("dp", "tensor"), None),
        P(),
        P(("dp", "expert")),
        P(("dp", "expert")),
        P(("dp", "expert")),
    )
    out_specs = (P(("dp", "expert"), None), P(("dp", "expert")))
    shape = mesh.shape
    rings = shape["dp"] == RING and shape["expert"] == RING and shape["tensor"] == 2
    body = per_device if rings else per_device_plain
    return jax.shard_map(
        body, mesh=mesh, in_specs=in_specs, out_specs=out_specs, check_vma=False
    )
```

time: 61.7 us -> 53.8 us (0.87)
  Pallas kernels: 56.9 us -> 50.3 us
  local copies, waits for them, and re-layouts: 3.88 us -> 2.66 us
    pallas_call x1, Pallas kernels: 56.9 us -> 50.3 us  [per_device(): pl.pallas_call(critic_kernel, out_shape=jax.ShapeDtypeStruct((rows + 8, a...]
    unnamed x2 -> x0, local copies, waits for them, and re-layouts: 2.59 us -> none
    slice x0 -> x1, local copies, waits for them, and re-layouts: none -> 1.47 us  [per_device(): return (outcome[:rows], outcome[rows])]
    reshape x1 -> x0, local copies, waits for them, and re-layouts: 1.29 us -> none  [per_device(): norm_gain.reshape(1, -1)]
    squeeze x0 -> x1, local copies, waits for them, and re-layouts: none -> 1.19 us  [per_device(): return (outcome[:rows], outcome[rows])]
where the time goes in v2:
time: 53.8 us; the launch traced here: 53.6 us
  Pallas kernels  50.3 us (93%)
  local copies, waits for them, and re-layouts  2.66 us (5%)
  between operations  0.64 us (1%)
    pallas_call x1, Pallas kernels, per_device(): pl.pallas_call(critic_kernel, out_shape=jax.ShapeDtypeStruct((rows + 8, a...  50.3 us
    slice x1, local copies, waits for them, and re-layouts, per_device(): return (outcome[:rows], outcome[rows])  1.47 us
    squeeze x1, local copies, waits for them, and re-layouts, per_device(): return (outcome[:rows], outcome[rows])  1.19 us

profile of v2, /device:TPU:1, one launch (start us, length us, event | category | flops | bytes accessed | tf_op | source)
XLA Modules:
  0.0 53.6 jit_solution(7528051634983779574)
XLA Ops:
  0.6 50.3 %shard_map.122 = f32[136,128]{1,0:T(8,128)} custom-call(bf16[128,1024]{1,0:T(8,128)(2,1)} %tokens_ref.1, bf16[16,128]{1,0:T(8,128)(2,1)} %bitcast.8, s32[2,128]{1,0:T(2,128)} %bitcast.9, s32[2,128]{1,0:T(2,128)} %bitcast.10, bf16[1,896,2048]{2,1,0:T(8,128)(2,1)} %gate_ref.1, bf16[1,896,2048]{2,1,0:T(8,128)(2,1)} %up_ref.1, bf16[1,896,2048]{2,1,0:T(8,128)(2,1)} %down_ref.1, ...), custom_call_target="tpu_custom_call" | custom-call | tf_op jit(solution)/shard_map/pallas_call | solution.py:751
  50.9 1.2 %slice_bitcast_fusion = f32[128]{0:T(128)} fusion(f32[136,128]{1,0:T(8,128)} %shard_map.122), kind=kLoop, calls=%fused_computation | loop fusion | bytes 1024 | tf_op jit(solution)/shard_map/squeeze | solution.py:805
  52.1 1.5 %slice.6 = f32[128,128]{1,0:T(8,128)} slice(f32[136,128]{1,0:T(8,128)} %shard_map.122), slice={[0:128], [0:128]} | slice | bytes 131072 | tf_op jit(solution)/shard_map/slice | solution.py:805

commit v3 on v2

--- a/solution.py
+++ b/solution.py
@@ -102,15 +102,14 @@
     ((1, 0, "F"),),
     ((0, 3, "W"), (0, 1, "W")),
     ((0, 2, "W"), (2, 0, "F")),
-    ((1, 3, "F"), (1, 1, "F"), (1, 0, "N"), (1, 3, "N")),
-    ((1, 2, "F"), (3, 0, "F"), (2, 0, "N")),
-    ((2, 3, "F"), (2, 1, "F"), (2, 3, "N")),
-    ((2, 2, "F"), (3, 0, "N"), (3, 3, "N"), (3, 1, "N")),
-    ((3, 3, "F"), (3, 1, "F"), (3, 2, "N")),
-    ((3, 2, "F"), (2, 1, "N"), (2, 2, "N")),
-    ((1, 1, "N"), (1, 2, "N")),
+    ((1, 3, "F"), (1, 1, "F"), (1, 0, "N")),
+    ((2, 3, "F"), (2, 1, "F"), (3, 0, "F")),
+    ((2, 2, "F"), (1, 3, "N"), (2, 0, "N"), (2, 3, "N"), (3, 0, "N")),
+    ((3, 3, "F"), (3, 1, "F"), (3, 3, "N")),
+    ((3, 2, "F"), (3, 1, "N"), (3, 2, "N")),
+    ((1, 2, "F"), (2, 1, "N"), (2, 2, "N"), (1, 1, "N"), (1, 2, "N")),
 )
-GROUPS = ((0, 1, 2), (3, 4), (5, 6), (7, 8), (9,), (10,))
+GROUPS = ((0, 1, 2), (3, 4), (5, 6), (7,), (8,), (9,))
 STRAIGHT = (4, 5)
 
 
@@ -127,9 +126,6 @@
     up_ref,
     down_ref,
     head_hbm,
-    actions_hbm,
-    rewards_hbm,
-    trace_hbm,
     outcome_ref,
     raw,
     gain_ref,
@@ -137,9 +133,6 @@
     ids_ref,
     codes_ref,
     head_ref,
-    actions_ref,
-    rewards_ref,
-    trace_ref,
     held,
     gate_buf,
     up_buf,
@@ -203,9 +196,6 @@
             (
                 (ids_hbm, ids_ref),
                 (codes_hbm, codes_ref),
-                (actions_hbm, actions_ref),
-                (rewards_hbm, rewards_ref),
-                (trace_hbm, trace_ref),
             )
         )
     ]
@@ -323,6 +313,10 @@
     def take(step, step_f, kind):
         arrive(step, step_f, kind)
         swap(step, step_f, kind)
+
+    def second_halves(step):
+        around(step, 0, "B", 1)
+        around(step, 0, "A", 3)
 
     first_axis = lax.broadcasted_iota(jnp.int32, (rows, rows), 0)
     second_axis = lax.broadcasted_iota(jnp.int32, (rows, rows), 1)
@@ -371,6 +365,7 @@
 
     around(0, 0, "A", 1)
     around(0, 0, "B", 3)
+    second_halves(0)
     inwards(0, 0, "B")
     only("end", lambda: inwards(0, 0, "N"))
     only("inner", lambda: outwards(0, 0, "B"))
@@ -398,6 +393,7 @@
             if before < number
             for _, _, kind in CHUNKS[before]
         )
+        bank = next(at for at, members in enumerate(GROUPS) if number in members) % 2
         parts = [
             (planes[step], (p + step_f) % RING, *spans[kind])
             for step, step_f, kind in CHUNKS[number]
@@ -422,7 +418,7 @@
             both = jnp.dot(
                 lhs, turned[:, 2 * at : 2 * at + 2 * TILE], preferred_element_type=jnp.float32
             )
-            hidden_buf[base : base + count, at : at + TILE] = (
+            hidden_buf[bank, base : base + count, at : at + TILE] = (
                 jax.nn.silu(both[:, :TILE]) * both[:, TILE:]
             ).astype(jnp.bfloat16)
 
@@ -433,7 +429,7 @@
         items = items_of(number)
         count = sum(height(kind) for _, _, kind in items)
         result = jnp.dot(
-            hidden_buf[:count, :], scored_buf[...], preferred_element_type=jnp.float32
+            hidden_buf[number % 2, :count, :], scored_buf[...], preferred_element_type=jnp.float32
         )
         result = result[:, :actions_count] + result[:, actions_count:]
         offset, target = 0, 0
@@ -524,10 +520,6 @@
         around(step, 0, "A", 1)
         around(step, 0, "B", 3)
 
-    def second_halves(step):
-        around(step, 0, "B", 1)
-        around(step, 0, "A", 3)
-
     def take_pair(step):
         arrive_both(step, 3, "B")
         swap(step, 3, "B")
@@ -547,39 +539,49 @@
             scored - high.astype(jnp.float32)
         ).astype(jnp.bfloat16)
 
+    def catch(step):
+        arrive_both(step, 3, "A")
+        swap(step, 3, "A")
+        swap(step, 1, "B")
+
     tiles = hidden_units // TILE
     load_gate.wait()
     load_up.wait()
     for tile in range(tiles):
         turn(tile)
+    chunk(0)
     for step_f, by, kind in ((3, 1, "a"), (1, 3, "b")):
         arrive(0, step_f, "N")
         around(0, step_f, kind, by)
         only("end", lambda: inwards(0, step_f, "N"))
         swap(0, step_f, "N")
-    second_halves(0)
     pass_far("A", 1, 3)
     only("end", lambda: take(1, 0, "A"))
-    chunk(0)
-    forward(0)
-    pass_far("B", 1, 3)
-
-    def pass_own():
-        for step_f in (0, 3):
-            outwards(0, step_f, "N")
-            inwards(0, step_f, "N")
-
-    only("inner", pass_own)
-    only("end", lambda: take(1, 0, "B"))
     load_down.wait()
     load_head.wait()
     score(0, tiles // 2 * TILE)
+    forward(0)
+    pass_far("B", 1, 3)
+
+    def pass_own():
+        outwards(0, 0, "N")
+        inwards(0, 0, "N")
+        inwards(0, 3, "N")
+
+    only("inner", pass_own)
+    only("end", lambda: take(1, 0, "B"))
+    first_halves(1)
+    second_halves(1)
+    score(tiles // 2 * TILE, hidden_units)
     arrive(0, 2, "N")
     only("end", lambda: inwards(0, 2, "N"))
     swap(0, 2, "N")
-    first_halves(1)
-    second_halves(1)
-    score(tiles // 2 * TILE, hidden_units)
+
+    def pass_early():
+        relay(1, 0, inwards)
+        inwards(0, 1, "N")
+
+    only("inner", pass_early)
     take_pair(0)
     pass_far("A", 2)
     only("end", lambda: take(2, 0, "A"))
@@ -588,81 +590,70 @@
     pass_far("B", 2)
     only("end", lambda: take(2, 0, "B"))
     first_halves(2)
-    relay_near(inwards, (1, 0), (1, 3))
+    second_halves(2)
+    relay_near(inwards, (1, 3))
     chunk(2)
-    forward(1)
-    second_halves(2)
+    catch(1)
 
     def pass_more():
+        outwards(0, 3, "N")
+        outwards(0, 1, "N")
         relay(1, 1, inwards)
         relay(1, 2, inwards)
-        inwards(0, 1, "N")
         inwards(0, 2, "N")
         relay(3, 0, outwards)
         relay(3, 3, outwards)
 
     only("inner", pass_more)
-    take_near((1, 0), (1, 3))
+    take_near((1, 0))
+    chunk(3)
+    only("end", lambda: take(3, 0, "A"))
+    around(3, 0, "A", 1)
+    take_pair(1)
+    relay_near(outwards, (2, 0))
     results(0)
-    chunk(3)
-    take_pair(1)
-    relay_near(outwards, (2, 0), (2, 3))
-    only("end", lambda: take(3, 0, "A"))
-    give_back(0)
+    forward(2)
     only("end", lambda: take(3, 0, "B"))
-    first_halves(3)
-    forward(2)
+    around(3, 0, "B", 3)
     second_halves(3)
     chunk(4)
-    relay_near(outwards, (2, 1), (2, 2))
-    take_last(1)
-    take_near((2, 0))
+    give_back(0)
+    relay_near(outwards, (2, 3))
+    take_pair(2)
     results(1)
-    take_pair(2)
-    take_near((2, 3))
 
     def pass_last():
+        relay(2, 1, outwards)
+        relay(2, 2, outwards)
         relay(3, 1, outwards)
         relay(3, 2, outwards)
-        outwards(0, 1, "N")
         outwards(0, 2, "N")
 
+    chunk(5)
     only("inner", pass_last)
-    chunk(5)
+    forward(3)
+    around(1, 3, "A", 1)
+    around(1, 1, "B", 3)
+    take_last(2)
+    take_near((2, 0), (1, 3), (2, 3), (3, 0))
     give_back(1)
-    forward(3)
-    take_near((3, 0), (3, 3), (3, 1))
     chunk(6)
-    take_last(2)
+    take_pair(3)
+    take_near((3, 3))
     results(2)
-    take_pair(3)
-    take_near((3, 2))
+    take_last(3)
+    take_near((3, 1), (3, 2))
     chunk(7)
+    results(3)
     give_back(2)
-    take_last(3)
+    take_last(1)
     take_near((2, 1), (2, 2))
     chunk(8)
-    take_near((1, 1), (1, 2))
-    results(3)
-    chunk(9)
     results(4)
     give_back(3)
-    chunk(10)
+    take_near((1, 1), (1, 2))
+    chunk(9)
     results(5)
-
-    trace_row = trace_ref[...].astype(jnp.float32) / 1024.0
-    trace_col = column(trace_row)
-    reward_col = column(rewards_ref[...].astype(jnp.float32) * 0.25)
-    action_col = column(actions_ref[...].astype(jnp.float32))
-    log_row = jnp.log(DISCOUNT * trace_row)
-    log_col = column(log_row)
-    sums_row = jnp.sum(jnp.where(first_axis <= second_axis, log_col, 0.0), axis=0, keepdims=True)
-    sums_col = jnp.sum(jnp.where(second_axis <= first_axis, log_row, 0.0), axis=1, keepdims=True)
-    weight = jnp.where(
-        first_axis >= second_axis, jnp.exp(jnp.minimum(sums_col - sums_row, 0.0)), 0.0
-    )
-    action_axis = lax.broadcasted_iota(jnp.int32, (rows, actions_count), 1).astype(jnp.float32)
-    chosen = action_axis == action_col
 
     straight = [
         (step, (-step_f) % RING, part)
@@ -701,7 +692,48 @@
         ],
         axis=0,
     )
-    outcome_ref[:rows, :] = values
+    outcome_ref[...] = values
+    for which in (None, "end", "inner"):
+        makes = [make for owner, make in sends if owner == which]
+
+        def finish(makes=makes):
+            for make in makes:
+                make().wait_send()
+
+        if which is None:
+            finish()
+        else:
+            pl.when(at_end if which == "end" else inner)(finish)
+
+
+def retrace_kernel(values_ref, actions_ref, rewards_ref, trace_ref, copied_ref, targets_ref):
+    values = values_ref[...]
+    copied_ref[...] = values
+    rows, actions_count = values.shape
+    first_axis = lax.broadcasted_iota(jnp.int32, (rows, rows), 0)
+    second_axis = lax.broadcasted_iota(jnp.int32, (rows, rows), 1)
+    same = first_axis == second_axis
+
+    def column(row):
+        return jnp.sum(jnp.where(same, row, 0.0), axis=1, keepdims=True)
+
+    def row_of(col):
+        return jnp.sum(jnp.where(same, col, 0.0), axis=0, keepdims=True)
+
+    trace_row = trace_ref[...].astype(jnp.float32) / 1024.0
+    trace_col = column(trace_row)
+    reward_col = column(rewards_ref[...].astype(jnp.float32) * 0.25)
+    action_col = column(actions_ref[...].astype(jnp.float32))
+    log_row = jnp.log(DISCOUNT * trace_row)
+    log_col = column(log_row)
+    sums_row = jnp.sum(jnp.where(first_axis <= second_axis, log_col, 0.0), axis=0, keepdims=True)
+    sums_col = jnp.sum(jnp.where(second_axis <= first_axis, log_row, 0.0), axis=1, keepdims=True)
+    weight = jnp.where(
+        first_axis >= second_axis, jnp.exp(jnp.minimum(sums_col - sums_row, 0.0)), 0.0
+    )
+    action_axis = lax.broadcasted_iota(jnp.int32, (rows, actions_count), 1).astype(jnp.float32)
+    chosen = action_axis == action_col
+
     greedy = jnp.max(values, axis=1, keepdims=True)
     taken = jnp.sum(jnp.where(chosen, values, 0.0), axis=1, keepdims=True)
     ahead_row = row_of(greedy - trace_col * taken)
@@ -709,19 +741,7 @@
         jnp.where(second_axis == first_axis + 1, ahead_row, 0.0), axis=1, keepdims=True
     )
     driver = reward_col + DISCOUNT * ahead
-    targets = jnp.sum(weight * driver, axis=0, keepdims=True)
-    outcome_ref[rows:, :] = jnp.broadcast_to(targets, (outcome_ref.shape[0] - rows, rows))
-    for which in (None, "end", "inner"):
-        makes = [make for owner, make in sends if owner == which]
-
-        def finish(makes=makes):
-            for make in makes:
-                make().wait_send()
-
-        if which is None:
-            finish()
-        else:
-            pl.when(at_end if which == "end" else inner)(finish)
+    targets_ref[...] = jnp.sum(weight * driver, axis=0, keepdims=True)
 
 
 def per_device(
@@ -750,8 +770,8 @@
     dma = pltpu.SemaphoreType.DMA
     outcome = pl.pallas_call(
         critic_kernel,
-        out_shape=jax.ShapeDtypeStruct((rows + 8, actions_count), jnp.float32),
-        in_specs=[hbm] * 11,
+        out_shape=jax.ShapeDtypeStruct((rows, actions_count), jnp.float32),
+        in_specs=[hbm] * 8,
         out_specs=vmem,
         scratch_shapes=[
             pltpu.VMEM((rows, wide), jnp.bfloat16),
@@ -760,16 +780,13 @@
             pltpu.VMEM((2, rows), jnp.int32),
             pltpu.VMEM((2, rows), jnp.int32),
             pltpu.VMEM((features, actions_count), jnp.bfloat16),
-            pltpu.VMEM((1, rows), jnp.int32),
-            pltpu.VMEM((1, rows), jnp.int32),
-            pltpu.VMEM((1, rows), jnp.int32),
             pltpu.VMEM((2, *blocks, rows, wide), jnp.bfloat16),
             pltpu.VMEM((hidden_units, features), jnp.bfloat16),
             pltpu.VMEM((hidden_units, features), jnp.bfloat16),
             pltpu.VMEM((hidden_units, features), jnp.bfloat16),
             pltpu.VMEM((features, 2 * hidden_units), jnp.bfloat16),
             pltpu.VMEM((hidden_units, 2 * actions_count), jnp.bfloat16),
-            pltpu.VMEM((most, hidden_units), jnp.bfloat16),
+            pltpu.VMEM((2, most, hidden_units), jnp.bfloat16),
             pltpu.VMEM((2, rows, TILE), jnp.float32),
             pltpu.VMEM((groups, 2, most // 2, actions_count), jnp.float32),
             pltpu.VMEM((groups, most // 2, actions_count), jnp.float32),
@@ -778,7 +795,7 @@
             pltpu.VMEM((2, RING * RING, far_half, actions_count), jnp.bfloat16),
             pltpu.VMEM((RING, rows, actions_count), jnp.float32),
             pltpu.VMEM((2, rows // 2, actions_count), jnp.float32),
-            dma((11,)),
+            dma((8,)),
             dma((1,)),
             dma((2,)),
             dma((RING, 9)),
@@ -798,11 +815,17 @@
         up_weights,
         down_weights,
         value_head,
-        actions.reshape(1, -1),
-        rewards.reshape(1, -1),
-        trace_codes.reshape(1, -1),
-    )
-    return outcome[:rows], outcome[rows]
+    )
+    values, targets = pl.pallas_call(
+        retrace_kernel,
+        out_shape=(
+            jax.ShapeDtypeStruct((rows, actions_count), jnp.float32),
+            jax.ShapeDtypeStruct((1, rows), jnp.float32),
+        ),
+        in_specs=[vmem] * 4,
+        out_specs=(vmem, vmem),
+    )(outcome, actions.reshape(1, -1), rewards.reshape(1, -1), trace_codes.reshape(1, -1))
+    return values, targets.reshape(-1)
 
 
 def solution(mesh):

time: 53.8 us -> 50.4 us (0.937)
  local copies, waits for them, and re-layouts: 2.66 us -> 0 us
  Pallas kernels: 50.3 us -> 49.5 us
    slice x1 -> x0, local copies, waits for them, and re-layouts: 1.47 us -> none  [per_device(): return (outcome[:rows], outcome[rows])]
    squeeze x1 -> x0, local copies, waits for them, and re-layouts: 1.19 us -> none  [per_device(): return (outcome[:rows], outcome[rows])]
    pallas_call x1 -> x2, Pallas kernels: 50.3 us -> 49.5 us  [the longest x1 47.8 us: per_device(): pl.pallas_call(critic_kernel, out_shape=jax.ShapeDtypeStruct((rows, actio...]
where the time goes in v3:
time: 50.4 us; the launch traced here: 50.1 us
  Pallas kernels  49.5 us (98%)
  between operations  0.64 us (1%)
    pallas_call x1, Pallas kernels, per_device(): pl.pallas_call(critic_kernel, out_shape=jax.ShapeDtypeStruct((rows, actio...  47.8 us
    pallas_call x1, Pallas kernels, per_device(): pl.pallas_call(retrace_kernel, out_shape=(jax.ShapeDtypeStruct((rows, act...  1.67 us

profile of v3, /device:TPU:1, one launch (start us, length us, event | category | flops | bytes accessed | tf_op | source)
XLA Modules:
  0.0 50.1 jit_solution(4140530598255834158)
XLA Ops:
  0.6 47.8 %shard_map.122.values_ref = f32[128,128]{1,0:T(8,128)} custom-call(bf16[128,1024]{1,0:T(8,128)(2,1)} %tokens_ref.1, bf16[16,128]{1,0:T(8,128)(2,1)} %bitcast.7, s32[2,128]{1,0:T(2,128)} %bitcast.8, s32[2,128]{1,0:T(2,128)} %bitcast.9, bf16[1,896,2048]{2,1,0:T(8,128)(2,1)} %gate_ref.1, bf16[1,896,2048]{2,1,0:T(8,128)(2,1)} %up_ref.1, ...), custom_call_target="tpu_custom_call" | custom-call | tf_op jit(solution)/shard_map/pallas_call | solution.py:771
  48.5 1.7 %shard_map.123 = (f32[128,128]{1,0:T(8,128)}, f32[1,128]{1,0:T(1,128)}) custom-call(f32[128,128]{1,0:T(8,128)} %shard_map.122.values_ref, s32[1,128]{1,0:T(1,128)} %bitcast.10, s32[1,128]{1,0:T(1,128)} %bitcast.11, s32[1,128]{1,0:T(1,128)} %bitcast.12), custom_call_target="tpu_custom_call" | custom-call | tf_op jit(solution)/shard_map/pallas_call | solution.py:819

commit v4 on v3

--- a/solution.py
+++ b/solution.py
@@ -620,7 +620,6 @@
     give_back(0)
     relay_near(outwards, (2, 3))
     take_pair(2)
-    results(1)
 
     def pass_last():
         relay(2, 1, outwards)
@@ -636,10 +635,11 @@
     around(1, 1, "B", 3)
     take_last(2)
     take_near((2, 0), (1, 3), (2, 3), (3, 0))
-    give_back(1)
+    results(1)
     chunk(6)
     take_pair(3)
     take_near((3, 3))
+    give_back(1)
     results(2)
     take_last(3)
     take_near((3, 1), (3, 2))

time: 50.4 us -> 50.3 us (level)
  no operation moved by 1% of the time
where the time goes in v4:
time: 50.3 us; the launch traced here: 50 us
  Pallas kernels  49.3 us (98%)
  between operations  0.64 us (1%)
    pallas_call x1, Pallas kernels, per_device(): pl.pallas_call(critic_kernel, out_shape=jax.ShapeDtypeStruct((rows, actio...  47.6 us
    pallas_call x1, Pallas kernels, per_device(): pl.pallas_call(retrace_kernel, out_shape=(jax.ShapeDtypeStruct((rows, act...  1.67 us

profile of v4, /device:TPU:1, one launch (start us, length us, event | category | flops | bytes accessed | tf_op | source)
XLA Modules:
  0.0 50.0 jit_solution(6357145178196406965)
XLA Ops:
  0.6 47.6 %shard_map.122.values_ref = f32[128,128]{1,0:T(8,128)} custom-call(bf16[128,1024]{1,0:T(8,128)(2,1)} %tokens_ref.1, bf16[16,128]{1,0:T(8,128)(2,1)} %bitcast.7, s32[2,128]{1,0:T(2,128)} %bitcast.8, s32[2,128]{1,0:T(2,128)} %bitcast.9, bf16[1,896,2048]{2,1,0:T(8,128)(2,1)} %gate_ref.1, bf16[1,896,2048]{2,1,0:T(8,128)(2,1)} %up_ref.1, ...), custom_call_target="tpu_custom_call" | custom-call | tf_op jit(solution)/shard_map/pallas_call | solution.py:771
  48.3 1.7 %shard_map.123 = (f32[128,128]{1,0:T(8,128)}, f32[1,128]{1,0:T(1,128)}) custom-call(f32[128,128]{1,0:T(8,128)} %shard_map.122.values_ref, s32[1,128]{1,0:T(1,128)} %bitcast.10, s32[1,128]{1,0:T(1,128)} %bitcast.11, s32[1,128]{1,0:T(1,128)} %bitcast.12), custom_call_target="tpu_custom_call" | custom-call | tf_op jit(solution)/shard_map/pallas_call | solution.py:819
